TPU v7x, 32 devices: a whole 2x2x4 slice. The times are simulated.
32 devices in a mesh: gx: 16 (over z, y, x), gy: 2 (over core).
Axes of the slice: x: 2, y: 2, z: 4, core: 2. Of those that a mesh axis runs over, the one named last changes fastest.
Arguments:
- operator: float32 [243, 32768], P(None, ('gx', 'gy')), may hold values from -0.6 to 10.6
- basis_u: float32 [144, 32768], P(None, ('gx', 'gy')), may hold values from -6 to 6
- basis_c: float32 [144, 32768], P(None, ('gx', 'gy')), may hold values from -6 to 6
- right_side: float32 [3, 32768], P(None, ('gx', 'gy')), may hold values from -16 to 16
- new_rows: int32 [32768], P(('gx', 'gy')), may hold values from 0 to 32767, as said below
Outputs:
- solution: float32 [3, 32768], P(None, ('gx', 'gy'))
- residual: float32 [3, 32768], P(None, ('gx', 'gy'))
Inputs may be any that keep to these rules, and one draw needn't show every extreme that they name: `new_rows`: each block row gets one new index (a permutation). Each device sends 0 to 64 of its old rows to each device, and each device both sends exactly 64 rows to some peer and receives exactly 64 rows from some peer.
All inputs are finite; a program needn't handle non-finite values.
Results may differ from a plain program's by a relative error of at most 0.0003.
Values sent between devices are 32-bit elements; how exact they have to be, the bound alone decides.
A program may use at most 64 MiB of HBM per device.

v0:
```python
import functools

import jax
import jax.numpy as jnp
from jax import lax
from jax.experimental import pallas as pl
from jax.experimental.pallas import tpu as pltpu
from jax.sharding import PartitionSpec as P

CY = 8
CZ = 128
F32 = jnp.float32
BF16 = jnp.bfloat16
HIGH = lax.Precision.HIGHEST
NT = (((1,), (1,)), ((), ()))


def round_up(n, m):
    return (n + m - 1) // m * m


class Plan:
    def __init__(self, nx, ny, rows, op_rows, basis_rows):
        self.nx, self.ny, self.rows = nx, ny, rows
        self.peers = nx * ny
        self.k = basis_rows // 3
        self.op_rows, self.basis_rows = op_rows, basis_rows
        self.cap = 2 * rows // self.peers
        self.fold = CZ // self.cap
        self.c0 = round_up(op_rows, 8)
        self.b0 = self.c0 + basis_rows
        self.tag = self.b0 + 3
        self.part = round_up(-(-(self.tag + 1) // self.fold), 8)
        self.width = round_up(self.part * self.fold, 16)
        self.part = self.width // self.fold
        self.nblk = 2 * rows // 256
        self.per_blk = 2 * self.fold
        self.tiles = (self.k + 2 + 7) // 8
        self.stride = max(1, self.peers // 8)


def kernel(
    pn, op_ref, u_ref, c_ref, b_ref, rrow_ref, sol_ref, res_ref,
    pay, hl, slot, ohp, xs, snd, got, xhl, oht, acc, new, uv,
    gpart, grs, gsnd, gfull, gm, ginv,
    hsnd, hrcv, mred, rsnd, rrcv, ulhs, usnd, urcv, utmp,
    bulk_s, bulk_r, rs_s, rs_r, ag_s, ag_r, h_s, h_r, red_s, red_r, u_s, u_r,
):
    gx, gy = lax.axis_index("gx"), lax.axis_index("gy")
    me = gx * pn.ny + gy
    peers, rows, k = pn.peers, pn.rows, pn.k

    def dev(p):
        return {"gx": lax.div(p, pn.ny), "gy": lax.rem(p, pn.ny)}

    def remote(src, dst, ssem, rsem, p):
        return pltpu.make_async_remote_copy(
            src_ref=src, dst_ref=dst, send_sem=ssem, recv_sem=rsem,
            device_id=dev(p), device_id_type=pl.DeviceIdType.MESH,
        )

    def others(body):
        def step(d, _):
            body(lax.rem(me + d, peers))
            return 0
        lax.fori_loop(1, peers, step, 0)

    barrier = pltpu.get_barrier_semaphore()
    others(lambda p: pl.semaphore_signal(
        barrier, inc=1, device_id=dev(p), device_id_type=pl.DeviceIdType.MESH))

    pay[0 : pn.op_rows, :] = op_ref[...]
    pay[pn.op_rows : pn.c0, :] = jnp.zeros((pn.c0 - pn.op_rows, rows), F32)
    pay[pn.c0 : pn.b0, :] = c_ref[...]
    pay[pn.b0 : pn.width, :] = jnp.zeros((pn.width - pn.b0, rows), F32)
    pay[pn.b0 : pn.tag, :] = b_ref[...]
    shift = rows.bit_length() - 1
    local = lax.bitwise_and(rrow_ref[...], rows - 1) + 1
    pay[pn.tag : pn.tag + 1, :] = local.astype(F32)

    gpart[...] = jnp.zeros(gpart.shape, F32)
    gram = jnp.zeros((k, k), F32)
    raw = jnp.zeros((1, k), F32)
    b8 = pay[pn.b0 : pn.b0 + 8, :]
    for a in range(3):
        ca = pay[pn.c0 + a * k : pn.c0 + (a + 1) * k, :]
        gram = gram + lax.dot_general(ca, ca, NT, precision=HIGH, preferred_element_type=F32)
        raw = raw + lax.dot_general(b8, ca, NT, precision=HIGH, preferred_element_type=F32)[a : a + 1]
    b3 = pay[pn.b0 : pn.tag, :]
    bb = jnp.sum(jnp.sum(b3 * b3, axis=1, keepdims=True), axis=0, keepdims=True)
    gpart[0:k, 0:k] = gram
    gpart[k : k + 1, 0:k] = raw
    gpart[k + 1 : k + 2, :] = jnp.broadcast_to(bb, (1, CZ))

    pl.semaphore_wait(barrier, peers - 1)

    def tile(t):
        return pl.ds(pl.multiple_of(t * 8, 8), 8)

    def rs_send(t, _):
        own = t * pn.stride

        @pl.when(me != own)
        def _():
            remote(gpart.at[tile(t), :], grs.at[me], rs_s.at[t], rs_r.at[me], own).start()
        return 0

    lax.fori_loop(0, pn.tiles, rs_send, 0)

    trow = lax.shift_right_logical(rrow_ref[...], shift)
    jrow = lax.broadcasted_iota(jnp.int32, (CZ, rows), 1)
    irow = lax.broadcasted_iota(jnp.int32, (CZ, rows), 0)

    diagonal = (
        lax.broadcasted_iota(jnp.int32, (CZ, CZ), 0) == lax.broadcasted_iota(jnp.int32, (CZ, CZ), 1)
    )

    def slots(i, _):
        at = pl.ds(pl.multiple_of(i * CZ, CZ), CZ)
        line = lax.shift_right_logical(rrow_ref[:, at], shift).astype(F32)
        tc = jnp.sum(jnp.where(diagonal, line, 0.0), axis=1, keepdims=True).astype(jnp.int32)
        before = jnp.logical_and(tc == trow, jrow < irow + i * CZ)
        rank = jnp.sum(jnp.where(before, 1.0, 0.0), axis=1, keepdims=True)
        slot[at, :] = jnp.broadcast_to(tc * pn.cap + rank.astype(jnp.int32), (CZ, CZ))
        return 0

    lax.fori_loop(0, rows // CZ, slots, 0)
    full = pay[...]
    hi = full.astype(BF16)
    hl[0 : pn.width, :] = hi
    hl[pn.width :, :] = (full - hi.astype(F32)).astype(BF16)

    lane = lax.broadcasted_iota(jnp.int32, (1, CZ), 1)
    block = lax.div(me, pn.per_blk)

    def spread(parts, q):
        out = None
        for j, value in enumerate(parts):
            amount = (j - q) * pn.cap % CZ
            moved = pltpu.roll(value, amount, 1) if amount else value
            out = moved if out is None else jnp.where(lane >= j * pn.cap, moved, out)
        return out

    def pack(it, _):
        gb = lax.rem(block + it, pn.nblk)
        for half in range(2):
            ids = lane + (gb * 256 + half * CZ)
            ohp[gb, :, half * CZ : (half + 1) * CZ] = jnp.where(slot[...] == ids, 1.0, 0.0).astype(BF16)
        oh = ohp[gb]
        xs[...] = jnp.dot(hl[0 : pn.width, :], oh, preferred_element_type=F32)
        xs[...] += jnp.dot(hl[pn.width :, :], oh, preferred_element_type=F32)
        for half in range(2):
            parts = [xs[j * pn.part : (j + 1) * pn.part, half * CZ : (half + 1) * CZ] for j in range(pn.fold)]
            for q in range(pn.fold):
                p = gb * pn.per_blk + half * pn.fold + q
                packet = spread(parts, q)

                @pl.when(p == me)
                def _():
                    got[p] = packet

                @pl.when(p != me)
                def _():
                    snd[p] = packet
                    remote(snd.at[p], got.at[me], bulk_s.at[p], bulk_r.at[me], p).start()
        return 0

    lax.fori_loop(0, 2, pack, 0)

    mine = lax.div(me, pn.stride)
    owner = jnp.logical_and(lax.rem(me, pn.stride) == 0, mine < pn.tiles)

    @pl.when(owner)
    def _():
        grs[me] = gpart[tile(mine), :]
        others(lambda p: remote(gpart.at[tile(0), :], grs.at[p], rs_s.at[0], rs_r.at[p], p).wait_recv())
        total = jnp.sum(grs[...], axis=0)
        gsnd[...] = total
        gfull[mine] = total
        others(lambda p: remote(gsnd, gfull.at[mine], ag_s.at[p], ag_r.at[mine], p).start())

    lax.fori_loop(2, pn.nblk, pack, 0)

    for y in range(CY):
        uv[pl.ds(y, pn.basis_rows, stride=CY), :] = u_ref[:, y * CZ : (y + 1) * CZ]
    mred[...] = jnp.zeros(mred.shape, F32)
    ginv[...] = jnp.zeros(ginv.shape, F32)

    def ag_wait(t, _):
        own = t * pn.stride

        @pl.when(me != own)
        def _():
            remote(gsnd, gfull.at[t], ag_s.at[0], ag_r.at[t], own).wait_recv()
        return 0

    lax.fori_loop(0, pn.tiles, ag_wait, 0)
    sums = gfull[...].reshape(pn.tiles * 8, CZ)
    gm[...] = sums[0:k]
    sub_k = lax.broadcasted_iota(jnp.int32, (k, 1), 0)

    def sweep(i, _):
        m = gm[...]
        row = gm[pl.ds(i, 1), :]
        at = lane == i
        col = jnp.sum(jnp.where(at, m, 0.0), axis=1, keepdims=True)
        pivot = jnp.sum(jnp.where(at, row, 0.0), axis=1, keepdims=True)
        scaled = jnp.where(at, 1.0, row) / pivot
        inner = jnp.where(at, 0.0, m) - col * scaled
        gm[...] = jnp.where(sub_k == i, scaled, inner)
        return 0

    lax.fori_loop(0, k, sweep, 0)
    ginv[0:k, :] = gm[...]

    def solve(p):
        return jnp.dot(p, ginv[...], precision=HIGH, preferred_element_type=F32)

    def bdot(p, z):
        return jnp.sum(jnp.where(lane < k, p * z, 0.0), axis=1, keepdims=True)

    s_row = jnp.broadcast_to(sums[k : k + 1, :], (8, CZ))
    bb_all = jnp.broadcast_to(sums[k + 1 : k + 2, 0:1], (8, 1))
    z0 = solve(s_row)
    beta = jnp.sqrt(bb_all - bdot(s_row, z0))

    acc[...] = jnp.zeros(acc.shape, F32)
    sub_r = lax.broadcasted_iota(jnp.int32, (rows, 1), 0).astype(F32) + 1.0

    half_n = pn.nblk // 2

    def unpack(it, _):
        far = lax.div(it, half_n)
        side = lax.rem(lax.div(block, half_n) + far, 2)
        start = jnp.where(far == 0, block, half_n - 1)
        gb = side * half_n + lax.rem(start - it + 2 * pn.nblk, half_n)
        for half in range(2):
            values = []
            for q in range(pn.fold):
                p = gb * pn.per_blk + half * pn.fold + q

                @pl.when(p != me)
                def _():
                    remote(snd.at[p], got.at[p], bulk_s.at[p], bulk_r.at[p], p).wait_recv()
            for q in range(pn.fold):
                values.append(got[gb * pn.per_blk + half * pn.fold + q])
            for j in range(pn.fold):
                xs[j * pn.part : (j + 1) * pn.part, half * CZ : (half + 1) * CZ] = spread(values, j)
            tags = xs[pn.tag : pn.tag + 1, half * CZ : (half + 1) * CZ]
            oht[gb, :, half * CZ : (half + 1) * CZ] = jnp.where(sub_r == tags, 1.0, 0.0).astype(BF16)
        x = xs[...]
        xh = x.astype(BF16)
        xhl[0 : pn.width, :] = xh
        xhl[pn.width :, :] = (x - xh.astype(F32)).astype(BF16)
        for n in range(rows // 256):
            at = slice(n * 256, (n + 1) * 256)
            o = oht[gb, at, :]
            acc[:, at] += lax.dot_general(xhl[0 : pn.width, :], o, NT, preferred_element_type=F32)
            acc[:, at] += lax.dot_general(xhl[pn.width :, :], o, NT, preferred_element_type=F32)
        return 0

    lax.fori_loop(0, pn.nblk, unpack, 0)

    def relayout(first, last):
        for y in range(CY):
            new[pl.ds(first * CY + y, last - first, stride=CY), :] = acc[first:last, y * CZ : (y + 1) * CZ]

    relayout(pn.c0, pn.width)

    def row(i):
        return new[i * CY : (i + 1) * CY, :]

    sub = lax.broadcasted_iota(jnp.int32, (CY, CZ), 0)
    lane8 = lax.broadcasted_iota(jnp.int32, (CY, CZ), 1)

    def combine(get, z):
        out = [jnp.zeros((CY, CZ), F32)] * 3
        for m in range(k):
            zb = jnp.broadcast_to(z[:, m : m + 1], (CY, CZ))
            for a in range(3):
                out[a] = out[a] + get(a * k + m) * zb
        return out

    def c_row(i):
        return row(pn.c0 + i)

    def u_row(i):
        return uv[i * CY : (i + 1) * CY, :]

    places = ((-1, 0), (1, 0), (0, 1), (-1, 1), (1, 1))

    def apply_op(phase, v, between=None):
        for b in range(3):
            hsnd[phase, b] = v[b]
        for j, (dx, oy) in enumerate(places):
            to = gx - dx
            target = to * pn.ny + (lax.rem(gy + oy, 2))

            @pl.when(jnp.logical_and(to >= 0, to < pn.nx))
            def _():
                remote(hsnd.at[phase], hrcv.at[phase, j], h_s.at[phase, j], h_r.at[phase, j], target).start()
        if between is not None:
            between()
        for j, (dx, oy) in enumerate(places):
            there = gx + dx
            source = there * pn.ny + (lax.rem(gy + oy, 2))
            valid = jnp.logical_and(there >= 0, there < pn.nx)

            @pl.when(valid)
            def _():
                remote(hsnd.at[phase], hrcv.at[phase, j], h_s.at[phase, j], h_r.at[phase, j], source).wait_recv()

            @pl.when(jnp.logical_not(valid))
            def _():
                hrcv[phase, j] = jnp.zeros((3, CY, CZ), F32)
        out = [jnp.zeros((CY, CZ), F32)] * 3
        for dx in (-1, 0, 1):
            for b in range(3):
                near = v[b] if dx == 0 else hrcv[phase, places.index((dx, 0)), b]
                side = hrcv[phase, places.index((dx, 1)), b]
                for dy in (-1, 0, 1):
                    if dy == 0:
                        moved = near
                    elif dy == -1:
                        edge = jnp.where(gy > 0, pltpu.roll(side, 1, 0), 0.0)
                        moved = jnp.where(sub == 0, edge, pltpu.roll(near, 1, 0))
                    else:
                        edge = jnp.where(gy == 0, pltpu.roll(side, CY - 1, 0), 0.0)
                        moved = jnp.where(sub == CY - 1, edge, pltpu.roll(near, CY - 1, 0))
                    for dz in (-1, 0, 1):
                        if dz == 0:
                            value = moved
                        elif dz == -1:
                            value = jnp.where(lane8 == 0, 0.0, pltpu.roll(moved, 1, 1))
                        else:
                            value = jnp.where(lane8 == CZ - 1, 0.0, pltpu.roll(moved, CZ - 1, 1))
                        kk = (dx + 1) * 9 + (dy + 1) * 3 + dz + 1
                        for a in range(3):
                            out[a] = out[a] + row((kk * 3 + a) * 3 + b) * value
        return out

    def put(i, value):
        mred[i : i + 1, :] = jnp.sum(value, axis=0, keepdims=True)

    def dot3(p, q):
        return p[0] * q[0] + p[1] * q[1] + p[2] * q[2]

    def sums_of(phase, image, vectors):
        for m in range(k):
            put(m, dot3([c_row(a * k + m) for a in range(3)], image))
        for i, vector in enumerate(vectors + [image]):
            put(k + i, dot3(vector, image))
        mine_row = lax.dot_general(jnp.ones((8, CZ), F32), mred[...], NT, precision=HIGH, preferred_element_type=F32)[0:1]
        rsnd[phase] = mine_row
        rrcv[phase, me] = mine_row
        others(lambda p: remote(rsnd.at[phase], rrcv.at[phase, me], red_s.at[phase, p], red_r.at[phase, me], p).start())
        others(lambda p: remote(rsnd.at[phase], rrcv.at[phase, p], red_s.at[phase, p], red_r.at[phase, p], p).wait_recv())
        return jnp.broadcast_to(jnp.sum(rrcv[phase], axis=0), (8, CZ))

    load = [row(pn.b0 + a) for a in range(3)]
    part = combine(c_row, z0)
    v1 = [(load[a] - part[a]) / beta for a in range(3)]
    w = apply_op(0, v1, lambda: relayout(0, pn.c0))
    p1 = sums_of(0, w, [v1])
    z1 = solve(p1)
    h11, ww = p1[:, k : k + 1], p1[:, k + 1 : k + 2]
    h21 = jnp.sqrt(ww - bdot(p1, z1) - h11 * h11)
    part = combine(c_row, z1)
    v2 = [(w[a] - part[a] - h11 * v1[a]) / h21 for a in range(3)]
    w = apply_op(1, v2)
    p2 = sums_of(1, w, [v1, v2])
    z2 = solve(p2)
    h12, h22, ww = p2[:, k : k + 1], p2[:, k + 1 : k + 2], p2[:, k + 2 : k + 3]
    h32 = jnp.sqrt(ww - bdot(p2, z2) - h12 * h12 - h22 * h22)
    m11 = h11 * h11 + h21 * h21
    m12 = h11 * h12 + h21 * h22
    m22 = h12 * h12 + h22 * h22 + h32 * h32
    g_one, g_two = beta * h11, beta * h12
    determ = m11 * m22 - m12 * m12
    y_one = (m22 * g_one - m12 * g_two) / determ
    y_two = (m11 * g_two - m12 * g_one) / determ

    ut = combine(u_row, z0 - y_one * z1 - y_two * z2)
    for y in range(CY):
        tile_y = jnp.zeros((8, CZ), F32)
        for a in range(3):
            tile_y = jnp.where(sub == a, jnp.broadcast_to(ut[a][y : y + 1, :], (8, CZ)), tile_y)
        high = tile_y.astype(BF16).astype(F32)
        ulhs[0:8, y * CZ : (y + 1) * CZ] = high
        ulhs[8:16, y * CZ : (y + 1) * CZ] = tile_y - high
    ub = ulhs[...].astype(BF16)

    def upack(gb, _):
        d = jnp.dot(ub, ohp[gb], preferred_element_type=F32)
        d = d[0:8] + d[8:16]
        usnd[2 * gb] = d[0:4, :CZ]
        usnd[2 * gb + 1] = d[0:4, CZ:]
        return 0

    lax.fori_loop(0, pn.nblk, upack, 0)
    others(lambda p: remote(usnd.at[lax.div(p, pn.fold)], urcv.at[me], u_s.at[p], u_r.at[me], p).start())
    urcv[me] = usnd[lax.div(me, pn.fold)]
    others(lambda p: remote(usnd.at[0], urcv.at[p], u_s.at[p], u_r.at[p], p).wait_recv())
    place = lax.rem(me, pn.fold)
    utmp[...] = jnp.zeros(utmp.shape, F32)

    def uunpack(gb, total):
        halves = []
        for half in range(2):
            out = None
            for q in range(pn.fold):
                at = (half * pn.fold + q) * 8
                utmp[at : at + 4, :] = urcv[gb * pn.per_blk + half * pn.fold + q]
                tile_q = utmp[at : at + 8, :]
                if pn.fold > 1:
                    tile_q = pltpu.roll(tile_q, lax.rem((q - place) * pn.cap + CZ, CZ), 1)
                out = tile_q if out is None else jnp.where(lane >= q * pn.cap, tile_q, out)
            halves.append(out)
        x = jnp.concatenate(halves, axis=1)
        high = x.astype(BF16).astype(F32)
        x2 = jnp.concatenate([high, x - high], axis=0).astype(BF16)
        return total + lax.dot_general(x2, oht[gb], NT, preferred_element_type=F32)

    moved = lax.fori_loop(0, pn.nblk, uunpack, jnp.zeros((16, rows), F32))
    moved = moved[0:8] + moved[8:16]
    sol = []
    for a in range(3):
        value = jnp.zeros((CY, CZ), F32)
        for y in range(CY):
            line = jnp.broadcast_to(moved[a : a + 1, y * CZ : (y + 1) * CZ], (CY, CZ))
            value = jnp.where(sub == y, line, value)
        sol.append(value + y_one * v1[a] + y_two * v2[a])
        sol_ref[a] = sol[a]
    w = apply_op(2, sol)
    for a in range(3):
        res_ref[a] = row(pn.b0 + a) - w[a]

    def rs_done(t, _):
        own = t * pn.stride

        @pl.when(me != own)
        def _():
            remote(gpart.at[tile(t), :], grs.at[me], rs_s.at[t], rs_r.at[me], own).wait_send()
        return 0

    lax.fori_loop(0, pn.tiles, rs_done, 0)

    @pl.when(owner)
    def _():
        others(lambda p: remote(gsnd, gfull.at[mine], ag_s.at[p], ag_r.at[mine], p).wait_send())

    others(lambda p: remote(snd.at[p], got.at[me], bulk_s.at[p], bulk_r.at[me], p).wait_send())
    for phase in range(2):
        others(lambda p: remote(rsnd.at[phase], rrcv.at[phase, me], red_s.at[phase, p], red_r.at[phase, me], p).wait_send())
    others(lambda p: remote(usnd.at[lax.div(p, pn.fold)], urcv.at[me], u_s.at[p], u_r.at[me], p).wait_send())
    for phase in range(3):
        for j, (dx, oy) in enumerate(places):
            to = gx - dx
            target = to * pn.ny + (lax.rem(gy + oy, 2))

            @pl.when(jnp.logical_and(to >= 0, to < pn.nx))
            def _():
                remote(hsnd.at[phase], hrcv.at[phase, j], h_s.at[phase, j], h_r.at[phase, j], target).wait_send()


def body(nx, ny, operator, basis_u, basis_c, right_side, new_rows):
    rows = operator.shape[1]
    pn = Plan(nx, ny, rows, operator.shape[0], basis_u.shape[0])
    n = pn.peers
    vmem, dma = pltpu.VMEM, pltpu.SemaphoreType.DMA
    out = jax.ShapeDtypeStruct((3, CY, CZ), F32)
    whole = pl.BlockSpec(memory_space=pltpu.VMEM)
    sol, res = pl.pallas_call(
        functools.partial(kernel, pn),
        out_shape=(out, out),
        in_specs=[whole] * 5,
        out_specs=(whole, whole),
        scratch_shapes=[
            vmem((pn.width, rows), F32),
            vmem((2 * pn.width, rows), BF16),
            vmem((rows, CZ), jnp.int32),
            vmem((pn.nblk, rows, 256), BF16),
            vmem((pn.width, 256), F32),
            vmem((n, pn.part, CZ), F32),
            vmem((n, pn.part, CZ), F32),
            vmem((2 * pn.width, 256), BF16),
            vmem((pn.nblk, rows, 256), BF16),
            vmem((pn.width, rows), F32),
            vmem((pn.width * CY, CZ), F32),
            vmem((pn.basis_rows * CY, CZ), F32),
            vmem((pn.tiles * 8, CZ), F32),
            vmem((n, 8, CZ), F32),
            vmem((8, CZ), F32),
            vmem((pn.tiles, 8, CZ), F32),
            vmem((pn.k, CZ), F32),
            vmem((CZ, CZ), F32),
            vmem((3, 3, CY, CZ), F32),
            vmem((3, 5, 3, CY, CZ), F32),
            vmem((CZ, CZ), F32),
            vmem((2, 1, CZ), F32),
            vmem((2, n, 1, CZ), F32),
            vmem((16, rows), F32),
            vmem((2 * pn.nblk, 4, CZ), F32),
            vmem((n, 4, CZ), F32),
            vmem((pn.per_blk * 8, CZ), F32),
            dma((n,)), dma((n,)),
            dma((pn.tiles,)), dma((n,)),
            dma((n,)), dma((pn.tiles,)),
            dma((3, 5)), dma((3, 5)),
            dma((2, n)), dma((2, n)),
            dma((n,)), dma((n,)),
        ],
        compiler_params=pltpu.CompilerParams(
            collective_id=0, has_side_effects=True, vmem_limit_bytes=60 << 20
        ),
        name="solve",
    )(operator, basis_u, basis_c, right_side, new_rows.reshape(1, rows))
    return sol.reshape(3, rows), res.reshape(3, rows)


def solution(mesh):
    split = P(None, ("gx", "gy"))
    return jax.shard_map(
        functools.partial(body, mesh.shape["gx"], mesh.shape["gy"]),
        mesh=mesh,
        in_specs=(split, split, split, split, P(("gx", "gy"))),
        out_specs=(split, split),
        check_vma=False,
    )
```

profile of v0, /device:TPU:1, one launch (start us, length us, event | category | flops | bytes accessed | tf_op | source)
XLA Modules:
  0.0 131.7 jit_solution(3980210188096981599)
XLA Ops:
  0.6 129.7 %solve.1 = (f32[3,8,128]{2,1,0:T(8,128)}, f32[3,8,128]{2,1,0:T(8,128)}) custom-call(f32[243,1024]{1,0:T(8,128)} %op_ref.1, f32[144,1024]{1,0:T(8,128)} %u_ref.1, f32[144,1024]{1,0:T(8,128)} %c_ref.1, f32[3,1024]{1,0:T(4,128)} %b_ref.1, s32[1,1024]{1,0:T(1,128)} %bitcast.9), custom_call_target="tpu_custom_call" | custom-call | tf_op jit(solution)/shard_map/solve/pallas_call | solution.py:473
  130.4 1.3 %copy_bitcast_fusion = (f32[3,1024]{1,0:T(4,128)}, f32[3,1024]{1,0:T(4,128)}) fusion(f32[1,3,8,128]{3,2,1,0:T(8,128)} %bitcast.8, f32[1,3,8,128]{3,2,1,0:T(8,128)} %bitcast.7), kind=kLoop, calls=%fused_computation | loop fusion | bytes 49152 | tf_op jit(solution)/shard_map/reshape | solution.py:518
where the time goes:
time: 133 us; the launch traced here: 132 us
  Pallas kernels  130 us (98%)
  local copies, waits for them, and re-layouts  1.34 us (1%)
    pallas_call x1, Pallas kernels, body(): pl.pallas_call(functools.partial(kernel, pn), out_shape=(out, out), in_sp...  130 us

commit v1 on v0

v1 whole, which is shorter than its diff:
```python
import functools

import jax
import jax.numpy as jnp
from jax import lax
from jax.experimental import pallas as pl
from jax.experimental.pallas import tpu as pltpu
from jax.sharding import PartitionSpec as P

LN = 128
F32 = jnp.float32
BF16 = jnp.bfloat16
I32 = jnp.int32
HIGH = lax.Precision.HIGHEST
NT = (((1,), (1,)), ((), ()))


class Plan:
    def __init__(self, nx, ny, rows, op_rows, basis_rows):
        self.nx, self.ny, self.rows = nx, ny, rows
        self.peers = nx * ny
        self.k = basis_rows // 3
        self.op_rows, self.basis_rows = op_rows, basis_rows
        self.lines = rows // LN
        self.q = nx * self.lines
        self.qh = self.q // 2
        self.cols = self.peers * self.lines
        self.blocks = self.cols // 256
        self.height = ny * self.lines


def kernel(
    pn, op_ref, u_ref, c_ref, b_ref, nr_ref, sol_ref, res_ref,
    opd, bd, nrb, iacc, itab, kidx, qidx, tab, wd, gpk, grcv, mred, rsnd, rrcv, vsnd, vb,
    n_s, n_r, g_s, g_r, r_s, r_r, v_s, v_r,
):
    gx, gy = lax.axis_index("gx"), lax.axis_index("gy")
    me = gx * pn.ny + gy
    peers, k, lines = pn.peers, pn.k, pn.lines

    def dev(p):
        return {"gx": lax.div(p, pn.ny), "gy": lax.rem(p, pn.ny)}

    def remote(src, dst, ssem, rsem, p):
        return pltpu.make_async_remote_copy(
            src_ref=src, dst_ref=dst, send_sem=ssem, recv_sem=rsem,
            device_id=dev(p), device_id_type=pl.DeviceIdType.MESH,
        )

    def others(body):
        def step(d, _):
            body(lax.rem(me + d, peers))
            return 0
        lax.fori_loop(1, peers, step, 0)

    barrier = pltpu.get_barrier_semaphore()
    others(lambda p: pl.semaphore_signal(
        barrier, inc=1, device_id=dev(p), device_id_type=pl.DeviceIdType.MESH))

    lane = lax.broadcasted_iota(I32, (8, LN), 1)
    sub = lax.broadcasted_iota(I32, (8, LN), 0)
    iota_row = lax.broadcasted_iota(I32, (256, LN), 0).astype(F32).astype(BF16)
    one, zero = jnp.ones((), BF16), jnp.zeros((), BF16)

    def lsum(x):
        return jnp.sum(x, axis=1, keepdims=True)

    def ssum(x):
        return jnp.sum(x, axis=0, keepdims=True)

    def fold(v):
        for h in (4, 2, 1):
            low = (sub & h) == 0
            n = len(v) // 2
            nxt = []
            for i in range(n):
                keep = jnp.where(low, v[i], v[i + n])
                give = jnp.where(low, v[i + n], v[i])
                if h == 4:
                    moved = pltpu.roll(give, 4, 0)
                else:
                    moved = jnp.where(low, pltpu.roll(give, 8 - h, 0), pltpu.roll(give, h, 0))
                nxt.append(keep + moved)
            v = nxt
        return v[0]

    def pick(parts, bits):
        for bit in bits:
            parts = [jnp.where(bit, parts[2 * j + 1], parts[2 * j]) for j in range(len(parts) // 2)]
        return parts[0]

    def onehot(row):
        return jnp.where(iota_row == row, one, zero)

    nrb[me] = nr_ref[...]

    ext = []
    for a in range(3):
        rows_b = jnp.broadcast_to(b_ref[a : a + 1, :], (8, pn.rows))
        ext.append(jnp.concatenate([c_ref[a * k : (a + 1) * k, :], rows_b], axis=0))
    gram = None
    for a in range(3):
        g = lax.dot_general(ext[a], ext[a], NT, precision=HIGH, preferred_element_type=F32)
        gram = g if gram is None else gram + g
    gram = jnp.concatenate([gram, jnp.zeros((k + 8, LN - k - 8), F32)], axis=1)
    lane16 = lax.broadcasted_iota(I32, (16, LN), 1)
    packet = jnp.zeros((16, LN), F32)
    third = k // 3
    groups = [gram[third * i : third * (i + 1)] for i in range(3)]
    tail = jnp.concatenate([gram[k : k + 8], gram[k : k + 8]], axis=0)
    starts = (0, third, 3 * third, 6 * third)
    for i in range(3):
        moved = pltpu.roll(groups[i], starts[i], 1) if starts[i] else groups[i]
        inside = jnp.logical_and(lane16 >= starts[i], lane16 < starts[i + 1])
        packet = jnp.where(inside, moved, packet)
        packet = jnp.where(lane16 == starts[3] + i, pltpu.roll(groups[i], starts[3] + i - k, 1), packet)
    packet = jnp.where(lane16 == starts[3] + 3, pltpu.roll(tail, starts[3] + 3 - k, 1), packet)
    gpk[...] = packet
    grcv[me] = packet

    pl.semaphore_wait(barrier, peers - 1)
    others(lambda p: remote(nr_ref, nrb.at[me], n_s.at[p], n_r.at[me], p).start())
    others(lambda p: remote(gpk, grcv.at[me], g_s.at[p], g_r.at[me], p).start())

    for t in range(lines):
        at = slice(t * LN, (t + 1) * LN)
        opd[pl.ds(t, pn.op_rows, stride=lines), :] = op_ref[:, at]
        bd[pl.ds(t, 3, stride=lines), :] = b_ref[:, at]
    load = [bd[a * lines : (a + 1) * lines, :] for a in range(3)]

    others(lambda p: remote(nr_ref, nrb.at[p], n_s.at[p], n_r.at[p], p).wait_recv())
    for cb in range(pn.blocks):
        iacc[cb] = jnp.zeros((256, 256), F32)
    lane_row = lax.broadcasted_iota(I32, (1, LN), 1)

    def invert(d, _):
        zs = []
        core = lax.rem(d, pn.ny)
        first = (core * LN + lane_row).astype(F32).astype(BF16)
        for s in range(lines):
            row = nrb[d, s : s + 1, :]
            zrow = lax.bitwise_and(row, LN - 1).astype(F32).astype(BF16)
            hit = iota_row[0:LN] == zrow
            line = lax.div(d, pn.ny) * lines + s - pn.qh
            second = jnp.full((1, LN), 0, I32) + line
            second = second.astype(F32).astype(BF16)
            zs.append(jnp.concatenate([jnp.where(hit, first, zero), jnp.where(hit, second, zero)], axis=0))
        z = jnp.concatenate(zs, axis=1)
        for cb in range(pn.blocks):
            cs = []
            for s in range(lines):
                crow = lax.shift_right_logical(nrb[d, s : s + 1, :], 7) - cb * 256
                crow = jnp.clip(crow, -1, 256).astype(F32).astype(BF16)
                cs.append(onehot(crow))
            c = jnp.concatenate(cs, axis=1)
            iacc[cb] += lax.dot_general(z, c, NT, preferred_element_type=F32)
        return 0

    lax.fori_loop(0, peers, invert, 0)
    for cb in range(pn.blocks):
        itab[cb] = iacc[cb].astype(BF16)

    others(lambda p: remote(gpk, grcv.at[p], g_s.at[p], g_r.at[p], p).wait_recv())
    total = grcv[0]
    for d in range(1, peers):
        total = total + grcv[d]
    ke = k + 8
    lanes_e = lax.broadcasted_iota(I32, (ke, LN), 1)
    rows_e = lax.broadcasted_iota(I32, (ke, LN), 0)
    low = []
    for i in range(3):
        block = pltpu.roll(total, LN - starts[i], 1) if starts[i] else total
        block = jnp.where(lane16 < third * (i + 1), block, 0.0)
        load_col = pltpu.roll(total, LN - (starts[3] + i) + k, 1)
        low.append(jnp.where(lane16 == k, load_col, block))
    square = pltpu.roll(total, LN - (starts[3] + 3) + k, 1)
    low.append(jnp.where(lane16 == k, square, 0.0)[0:8])
    low.append(jnp.zeros((LN - ke, LN), F32))
    low = jnp.concatenate(low, axis=0)
    high = jnp.transpose(low)
    low, high = low[0:ke], high[0:ke]
    diag = lax.div(rows_e, third) == lax.div(lanes_e, third)
    lower = jnp.logical_or(diag, lanes_e <= rows_e)
    mat = jnp.where(jnp.logical_or(lower, lanes_e == k), low, high)
    mat = jnp.where(jnp.logical_and(rows_e == k, lanes_e < k), high, mat)
    for i in range(k):
        row = mat[i : i + 1, :]
        col = jnp.broadcast_to(mat[:, i : i + 1], (ke, LN))
        at = lanes_e == i
        scaled = jnp.where(lane_row == i, 1.0, row) / col[i : i + 1]
        inner = jnp.where(at, 0.0, mat) - col * scaled
        mat = jnp.where(rows_e == i, scaled, inner)
    ginv = jnp.where(lanes_e < k, mat, 0.0)[0:k]
    z0 = jnp.broadcast_to(mat[0:k, k : k + 1], (k, LN))
    beta = jnp.sqrt(jnp.broadcast_to(mat[k : k + 1, k : k + 1], (1, LN)))

    def combine(ref, z):
        out = []
        for a in range(3):
            sums = []
            for t in range(lines):
                s = None
                for g in range(k // 8):
                    term = ref[a * k + 8 * g : a * k + 8 * g + 8, t * LN : (t + 1) * LN] * z[8 * g : 8 * g + 8]
                    s = term if s is None else s + term
                sums.append(s)
            out.append(fold(sums))
        return out

    half_n = pn.nx // 2
    side = lax.div(gx, half_n)

    def spread(phase, v):
        for a in range(3):
            vsnd[phase, a] = v[a]
            vb[phase, gy, a, pl.ds(pl.multiple_of(gx * lines, 8), 8), :] = v[a]
        mine = pl.ds(pl.multiple_of(gx * lines, 8), 8)
        others(lambda p: remote(
            vsnd.at[phase], vb.at[phase, gy, :, mine, :], v_s.at[phase, p], v_r.at[phase, me], p).start())

    def arrive(phase, half):
        def step(i, _):
            p = half * half_n * pn.ny + i
            at = pl.ds(pl.multiple_of(lax.div(p, pn.ny) * lines, 8), 8)

            @pl.when(p != me)
            def _():
                remote(vsnd.at[phase], vb.at[phase, lax.rem(p, pn.ny), :, at, :],
                       v_s.at[phase, p], v_r.at[phase, p], p).wait_recv()
            return 0
        lax.fori_loop(0, half_n * pn.ny, step, 0)
        begin = pl.ds(pl.multiple_of(half * pn.qh, 8), pn.qh)
        for b in range(3):
            for core in range(pn.ny):
                x = vb[phase, core, b, begin, :]
                hi = x.astype(BF16)
                lanes_c = slice(core * LN, (core + 1) * LN)
                tab[b * pn.qh : (b + 1) * pn.qh, lanes_c] = hi
                tab[(3 + b) * pn.qh : (4 + b) * pn.qh, lanes_c] = (x - hi.astype(F32)).astype(BF16)

    levels = pn.qh.bit_length() - 4
    rest = ~((pn.qh - 1) & ~7)

    def gather(kk, half):
        vals = [[None] * lines for _ in range(3)]
        for c in range(lines // 2):
            w = jnp.concatenate(
                [onehot(kidx[kk, 2 * c + t : 2 * c + t + 1, :].astype(BF16)) for t in range(2)], axis=1)
            r = jnp.dot(tab[...], w, preferred_element_type=F32)
            for t in range(2):
                q = jnp.broadcast_to(qidx[kk, 2 * c + t : 2 * c + t + 1, :], (8, LN)) - half * pn.qh
                bits = [lax.bitwise_and(q, 8 << i) != 0 for i in range(levels)]
                here = lax.bitwise_and(q, rest) == sub
                lanes_t = slice(t * LN, (t + 1) * LN)
                for b in range(3):
                    parts = []
                    for i in range(pn.qh // 8):
                        at = b * pn.qh + i * 8
                        lo = 3 * pn.qh + at
                        parts.append(r[at : at + 8, lanes_t] + r[lo : lo + 8, lanes_t])
                    vals[b][2 * c + t] = jnp.where(here, pick(parts, bits), 0.0)
        return [fold(vals[b]) for b in range(3)]

    def coef(i):
        return opd[pl.ds(pl.multiple_of(i * lines, 8), 8), :]

    def apply_half(half):
        def step(kk, out):
            g = gather(kk, half)
            return tuple(
                out[a] + coef(kk * 9 + a * 3) * g[0] + coef(kk * 9 + a * 3 + 1) * g[1] + coef(kk * 9 + a * 3 + 2) * g[2]
                for a in range(3))
        return lax.fori_loop(0, pn.op_rows // 9, step, (jnp.zeros((8, LN), F32),) * 3)

    def apply_op(phase, extra=False):
        def step(i, carry):
            half = lax.rem(side + i, 2)
            arrive(phase, half)
            part = apply_half(half)
            if extra:
                part = part + tuple(gather(pn.op_rows // 9, half))
            return tuple(x + y for x, y in zip(carry, part))
        return lax.fori_loop(0, 2, step, (jnp.zeros((8, LN), F32),) * (6 if extra else 3))

    def dot3(p, q):
        return ssum(p[0] * q[0] + p[1] * q[1] + p[2] * q[2])

    def sums_of(phase, w, vectors):
        for a in range(3):
            wd[a] = w[a]
        bc = [[jnp.broadcast_to(wd[a, t : t + 1, :], (8, LN)) for t in range(lines)] for a in range(3)]
        for g in range(k // 8):
            s = None
            for a in range(3):
                for t in range(lines):
                    term = c_ref[a * k + 8 * g : a * k + 8 * g + 8, t * LN : (t + 1) * LN] * bc[a][t]
                    s = term if s is None else s + term
            mred[8 * g : 8 * g + 8, :] = s
        tail_rows = jnp.zeros((8, LN), F32)
        for i, vector in enumerate(vectors + [w]):
            tail_rows = jnp.where(sub == i, dot3(vector, w), tail_rows)
        mred[k : k + 8, :] = tail_rows
        mred[k + 8 :, :] = jnp.zeros((LN - k - 8, LN), F32)
        mine_row = lax.dot_general(jnp.ones((8, LN), F32), mred[...], NT, precision=HIGH, preferred_element_type=F32)[0:1]
        rsnd[phase] = mine_row
        rrcv[phase, me] = mine_row
        others(lambda p: remote(rsnd.at[phase], rrcv.at[phase, me], r_s.at[phase, p], r_r.at[phase, me], p).start())
        others(lambda p: remote(rsnd.at[phase], rrcv.at[phase, p], r_s.at[phase, p], r_r.at[phase, p], p).wait_recv())
        prow = jnp.sum(rrcv[phase], axis=0)
        pcol = lsum(jnp.where(lanes_e == rows_e, prow, 0.0))
        z = lsum(ginv * prow)
        pz = ssum(pcol[0:k] * z)
        pcol = jnp.broadcast_to(pcol, (ke, LN))
        return jnp.broadcast_to(z, (k, LN)), jnp.broadcast_to(pz, (1, LN)), [pcol[k + i : k + i + 1] for i in range(3)]

    part = combine(c_ref, z0)
    v1 = [(load[a] - part[a]) / beta for a in range(3)]
    spread(0, v1)

    nr = nr_ref[...]
    x_at = lax.div(nr, pn.height * LN)
    y_at = lax.bitwise_and(lax.shift_right_logical(nr, 7), pn.height - 1)
    z_at = lax.bitwise_and(nr, LN - 1)
    zl = LN.bit_length() - 4

    def look(crow_of, zrow_of, shifts):
        vals = [[[None] * lines for _ in range(2)] for _ in shifts]
        for c in range(lines // 2):
            r = None
            for cb in range(pn.blocks):
                w = jnp.concatenate(
                    [onehot(jnp.clip(crow_of(2 * c + t) - cb * 256, -1, 256).astype(F32).astype(BF16)) for t in range(2)],
                    axis=1)
                d = jnp.dot(itab[cb], w, preferred_element_type=F32)
                r = d if r is None else r + d
            for t in range(2):
                for i, dz in enumerate(shifts):
                    zq = jnp.broadcast_to(zrow_of(2 * c + t), (8, LN)) + dz
                    bits = [lax.bitwise_and(zq, 8 << j) != 0 for j in range(zl)]
                    here = lax.bitwise_and(zq, 7) == sub
                    for p in range(2):
                        parts = [r[p * LN + 8 * j : p * LN + 8 * j + 8, t * LN : (t + 1) * LN] for j in range(LN // 8)]
                        vals[i][p][2 * c + t] = jnp.where(here, pick(parts, bits), 0.0)
        return [[fold(vals[i][p]) for p in range(2)] for i in range(len(shifts))]

    def neighbours(j, _):
        dx = lax.div(j, 3) - 1
        dy = lax.rem(j, 3) - 1
        found = look(
            lambda t: lax.shift_right_logical(nr_ref[t : t + 1, :], 7) + (dx * pn.height + dy),
            lambda t: lax.bitwise_and(nr_ref[t : t + 1, :], LN - 1),
            (-1, 0, 1))
        xs, ys = x_at + dx, y_at + dy
        inside = jnp.logical_and(
            jnp.logical_and(xs >= 0, xs < pn.nx), jnp.logical_and(ys >= 0, ys < pn.height))
        for i, dz in enumerate((-1, 0, 1)):
            zs = z_at + dz
            good = jnp.logical_and(inside, jnp.logical_and(zs >= 0, zs < LN))
            kidx[j * 3 + i] = found[i][0]
            qidx[j * 3 + i] = jnp.where(good, found[i][1].astype(I32) + pn.qh, -1)
        return 0

    lax.fori_loop(0, 9, neighbours, 0)
    own = look(
        lambda t: jnp.zeros((1, LN), I32) + (me * lines + t), lambda t: lane_row, (0,))
    kidx[pn.op_rows // 9] = own[0][0]
    qidx[pn.op_rows // 9] = own[0][1].astype(I32) + pn.qh

    w1 = apply_op(0)
    z1, pz, (h11, ww, _) = sums_of(0, w1, [v1])
    h21 = jnp.sqrt(ww - pz - h11 * h11)
    part = combine(c_ref, z1)
    v2 = [(w1[a] - part[a] - h11 * v1[a]) / h21 for a in range(3)]
    spread(1, v2)
    w2 = apply_op(1)
    z2, pz, (h12, h22, ww) = sums_of(1, w2, [v1, v2])
    h32 = jnp.sqrt(ww - pz - h12 * h12 - h22 * h22)
    m11 = h11 * h11 + h21 * h21
    m12 = h11 * h12 + h21 * h22
    m22 = h12 * h12 + h22 * h22 + h32 * h32
    g_one, g_two = beta * h11, beta * h12
    determ = m11 * m22 - m12 * m12
    y_one = (m22 * g_one - m12 * g_two) / determ
    y_two = (m11 * g_two - m12 * g_one) / determ
    ut = combine(u_ref, z0 - y_one * z1 - y_two * z2)
    spread(2, [ut[a] + y_one * v1[a] + y_two * v2[a] for a in range(3)])
    out = apply_op(2, extra=True)
    spread(3, [load[a] - out[a] for a in range(3)])
    for a in range(3):
        sol_ref[a] = out[3 + a]

    def last(i, carry):
        half = lax.rem(side + i, 2)
        arrive(3, half)
        return tuple(x + y for x, y in zip(carry, gather(pn.op_rows // 9, half)))

    out = lax.fori_loop(0, 2, last, (jnp.zeros((8, LN), F32),) * 3)
    for a in range(3):
        res_ref[a] = out[a]

    others(lambda p: remote(nr_ref, nrb.at[me], n_s.at[p], n_r.at[me], p).wait_send())
    others(lambda p: remote(gpk, grcv.at[me], g_s.at[p], g_r.at[me], p).wait_send())
    mine = pl.ds(pl.multiple_of(gx * lines, 8), 8)
    for phase in range(2):
        others(lambda p: remote(rsnd.at[phase], rrcv.at[phase, me], r_s.at[phase, p], r_r.at[phase, me], p).wait_send())
    for phase in range(4):
        others(lambda p: remote(
            vsnd.at[phase], vb.at[phase, gy, :, mine, :], v_s.at[phase, p], v_r.at[phase, me], p).wait_send())


def body(nx, ny, operator, basis_u, basis_c, right_side, new_rows):
    rows = operator.shape[1]
    pn = Plan(nx, ny, rows, operator.shape[0], basis_u.shape[0])
    n, lines = pn.peers, pn.lines
    vmem, dma = pltpu.VMEM, pltpu.SemaphoreType.DMA
    out = jax.ShapeDtypeStruct((3, lines, LN), F32)
    whole = pl.BlockSpec(memory_space=pltpu.VMEM)
    points = pn.op_rows // 9 + 1
    sol, res = pl.pallas_call(
        functools.partial(kernel, pn),
        out_shape=(out, out),
        in_specs=[whole] * 5,
        out_specs=(whole, whole),
        scratch_shapes=[
            vmem((pn.op_rows * lines, LN), F32),
            vmem((3 * lines, LN), F32),
            vmem((n, lines, LN), I32),
            vmem((pn.blocks, 256, 256), F32),
            vmem((pn.blocks, 256, 256), BF16),
            vmem((points, lines, LN), F32),
            vmem((points, lines, LN), I32),
            vmem((6 * pn.qh, 256), BF16),
            vmem((3, lines, LN), F32),
            vmem((16, LN), F32),
            vmem((n, 16, LN), F32),
            vmem((LN, LN), F32),
            vmem((2, 1, LN), F32),
            vmem((2, n, 1, LN), F32),
            vmem((4, 3, lines, LN), F32),
            vmem((4, ny, 3, pn.q, LN), F32),
            dma((n,)), dma((n,)),
            dma((n,)), dma((n,)),
            dma((2, n)), dma((2, n)),
            dma((4, n)), dma((4, n)),
        ],
        compiler_params=pltpu.CompilerParams(
            collective_id=0, has_side_effects=True, vmem_limit_bytes=60 << 20
        ),
        name="solve",
    )(operator, basis_u, basis_c, right_side, new_rows.reshape(lines, LN))
    return sol.reshape(3, rows), res.reshape(3, rows)


def solution(mesh):
    split = P(None, ("gx", "gy"))
    return jax.shard_map(
        functools.partial(body, mesh.shape["gx"], mesh.shape["gy"]),
        mesh=mesh,
        in_specs=(split, split, split, split, P(("gx", "gy"))),
        out_specs=(split, split),
        check_vma=False,
    )
```

time: 133 us -> 145 us (1.090)
  Pallas kernels: 130 us -> 142 us
    pallas_call x1, Pallas kernels: 130 us -> 142 us  [body(): pl.pallas_call(functools.partial(kernel, pn), out_shape=(out, out), in_sp...]
where the time goes in v1:
time: 145 us; the launch traced here: 144 us
  Pallas kernels  142 us (98%)
    pallas_call x1, Pallas kernels, body(): pl.pallas_call(functools.partial(kernel, pn), out_shape=(out, out), in_sp...  142 us

profile of v1, /device:TPU:1, one launch (start us, length us, event | category | flops | bytes accessed | tf_op | source)
XLA Modules:
  0.0 144.1 jit_solution(364357422640901060)
XLA Ops:
  0.6 142.1 %solve.1 = (f32[3,8,128]{2,1,0:T(8,128)}, f32[3,8,128]{2,1,0:T(8,128)}) custom-call(f32[243,1024]{1,0:T(8,128)} %op_ref.1, f32[144,1024]{1,0:T(8,128)} %u_ref.1, f32[144,1024]{1,0:T(8,128)} %c_ref.1, f32[3,1024]{1,0:T(4,128)} %b_ref.1, s32[8,128]{1,0:T(8,128)} %bitcast.9), custom_call_target="tpu_custom_call" | custom-call | tf_op jit(solution)/shard_map/solve/pallas_call | solution.py:419
  142.8 1.3 copy_bitcast_fusion

commit v2 on v1

--- a/solution.py
+++ b/solution.py
@@ -11,6 +11,7 @@
 F32 = jnp.float32
 BF16 = jnp.bfloat16
 I32 = jnp.int32
+F8 = jnp.float8_e4m3fn
 HIGH = lax.Precision.HIGHEST
 NT = (((1,), (1,)), ((), ()))
 
@@ -31,7 +32,7 @@
 
 def kernel(
     pn, op_ref, u_ref, c_ref, b_ref, nr_ref, sol_ref, res_ref,
-    opd, bd, nrb, iacc, itab, kidx, qidx, tab, wd, gpk, grcv, mred, rsnd, rrcv, vsnd, vb,
+    opd, bd, nrb, iacc, itab, kidx, qidx, tab, sinv, wd, gpk, grcv, mred, rsnd, rrcv, vsnd, vb,
     n_s, n_r, g_s, g_r, r_s, r_r, v_s, v_r,
 ):
     gx, gy = lax.axis_index("gx"), lax.axis_index("gy")
@@ -97,12 +98,16 @@
     ext = []
     for a in range(3):
         rows_b = jnp.broadcast_to(b_ref[a : a + 1, :], (8, pn.rows))
-        ext.append(jnp.concatenate([c_ref[a * k : (a + 1) * k, :], rows_b], axis=0))
+        pad = jnp.zeros((LN // 2 - k - 8, pn.rows), F32)
+        ext.append(jnp.concatenate([c_ref[a * k : (a + 1) * k, :], rows_b, pad], axis=0))
     gram = None
     for a in range(3):
-        g = lax.dot_general(ext[a], ext[a], NT, precision=HIGH, preferred_element_type=F32)
+        hi = ext[a].astype(BF16)
+        both = jnp.concatenate([hi, (ext[a] - hi.astype(F32)).astype(BF16)], axis=0)
+        g = lax.dot_general(both, both, NT, preferred_element_type=F32)
         gram = g if gram is None else gram + g
-    gram = jnp.concatenate([gram, jnp.zeros((k + 8, LN - k - 8), F32)], axis=1)
+    gram = gram[0 : LN // 2] + gram[LN // 2 :]
+    gram = gram + pltpu.roll(gram, LN // 2, 1)
     lane16 = lax.broadcasted_iota(I32, (16, LN), 1)
     packet = jnp.zeros((16, LN), F32)
     third = k // 3
@@ -128,12 +133,17 @@
         bd[pl.ds(t, 3, stride=lines), :] = b_ref[:, at]
     load = [bd[a * lines : (a + 1) * lines, :] for a in range(3)]
 
-    others(lambda p: remote(nr_ref, nrb.at[p], n_s.at[p], n_r.at[p], p).wait_recv())
     for cb in range(pn.blocks):
         iacc[cb] = jnp.zeros((256, 256), F32)
     lane_row = lax.broadcasted_iota(I32, (1, LN), 1)
 
-    def invert(d, _):
+    def invert_one(i):
+        d = lax.rem(me + i, peers)
+
+        @pl.when(i > 0)
+        def _():
+            remote(nr_ref, nrb.at[d], n_s.at[d], n_r.at[d], d).wait_recv()
+
         zs = []
         core = lax.rem(d, pn.ny)
         first = (core * LN + lane_row).astype(F32).astype(BF16)
@@ -154,9 +164,13 @@
                 cs.append(onehot(crow))
             c = jnp.concatenate(cs, axis=1)
             iacc[cb] += lax.dot_general(z, c, NT, preferred_element_type=F32)
+
+    def invert(j, _):
+        for i in range(4):
+            invert_one(4 * j + i)
         return 0
 
-    lax.fori_loop(0, peers, invert, 0)
+    lax.fori_loop(0, peers // 4, invert, 0)
     for cb in range(pn.blocks):
         itab[cb] = iacc[cb].astype(BF16)
 
@@ -215,8 +229,22 @@
             vsnd[phase, a] = v[a]
             vb[phase, gy, a, pl.ds(pl.multiple_of(gx * lines, 8), 8), :] = v[a]
         mine = pl.ds(pl.multiple_of(gx * lines, 8), 8)
-        others(lambda p: remote(
-            vsnd.at[phase], vb.at[phase, gy, :, mine, :], v_s.at[phase, p], v_r.at[phase, me], p).start())
+        half = half_n * pn.ny
+        at = me - side * half
+
+        def send(p):
+            remote(vsnd.at[phase], vb.at[phase, gy, :, mine, :], v_s.at[phase, p], v_r.at[phase, me], p).start()
+
+        def near(i, _):
+            send(side * half + lax.rem(at + i, half))
+            return 0
+
+        def far(i, _):
+            send((1 - side) * half + lax.rem(at + i, half))
+            return 0
+
+        lax.fori_loop(1, half, near, 0)
+        lax.fori_loop(0, half, far, 0)
 
     def arrive(phase, half):
         def step(i, _):
@@ -231,12 +259,18 @@
         lax.fori_loop(0, half_n * pn.ny, step, 0)
         begin = pl.ds(pl.multiple_of(half * pn.qh, 8), pn.qh)
         for b in range(3):
+            xs = [vb[phase, core, b, begin, :] for core in range(pn.ny)]
+            top = functools.reduce(jnp.maximum, [jnp.abs(x) for x in xs])
+            top = jnp.maximum(jnp.max(top, axis=1, keepdims=True), 1e-30)
+            scale = 240.0 / top
+            sinv[b * pn.qh : (b + 1) * pn.qh, :] = jnp.broadcast_to(top * (1.0 / 240.0), (pn.qh, LN))
             for core in range(pn.ny):
-                x = vb[phase, core, b, begin, :]
-                hi = x.astype(BF16)
-                lanes_c = slice(core * LN, (core + 1) * LN)
-                tab[b * pn.qh : (b + 1) * pn.qh, lanes_c] = hi
-                tab[(3 + b) * pn.qh : (4 + b) * pn.qh, lanes_c] = (x - hi.astype(F32)).astype(BF16)
+                x = xs[core] * scale
+                for piece in range(3):
+                    part = x.astype(F8)
+                    x = x - part.astype(F32)
+                    at = (piece * 3 + b) * pn.qh
+                    tab[at : at + pn.qh, core * LN : (core + 1) * LN] = part
 
     levels = pn.qh.bit_length() - 4
     rest = ~((pn.qh - 1) & ~7)
@@ -245,7 +279,7 @@
         vals = [[None] * lines for _ in range(3)]
         for c in range(lines // 2):
             w = jnp.concatenate(
-                [onehot(kidx[kk, 2 * c + t : 2 * c + t + 1, :].astype(BF16)) for t in range(2)], axis=1)
+                [onehot(kidx[kk, 2 * c + t : 2 * c + t + 1, :].astype(BF16)) for t in range(2)], axis=1).astype(F8)
             r = jnp.dot(tab[...], w, preferred_element_type=F32)
             for t in range(2):
                 q = jnp.broadcast_to(qidx[kk, 2 * c + t : 2 * c + t + 1, :], (8, LN)) - half * pn.qh
@@ -256,8 +290,8 @@
                     parts = []
                     for i in range(pn.qh // 8):
                         at = b * pn.qh + i * 8
-                        lo = 3 * pn.qh + at
-                        parts.append(r[at : at + 8, lanes_t] + r[lo : lo + 8, lanes_t])
+                        ps = [r[at + 3 * pn.qh * j : at + 3 * pn.qh * j + 8, lanes_t] for j in range(3)]
+                        parts.append((ps[0] + (ps[1] + ps[2])) * sinv[at : at + 8, :])
                     vals[b][2 * c + t] = jnp.where(here, pick(parts, bits), 0.0)
         return [fold(vals[b]) for b in range(3)]
 
@@ -265,12 +299,15 @@
         return opd[pl.ds(pl.multiple_of(i * lines, 8), 8), :]
 
     def apply_half(half):
-        def step(kk, out):
-            g = gather(kk, half)
-            return tuple(
-                out[a] + coef(kk * 9 + a * 3) * g[0] + coef(kk * 9 + a * 3 + 1) * g[1] + coef(kk * 9 + a * 3 + 2) * g[2]
-                for a in range(3))
-        return lax.fori_loop(0, pn.op_rows // 9, step, (jnp.zeros((8, LN), F32),) * 3)
+        def step(i, out):
+            for u in range(3):
+                kk = 3 * i + u
+                g = gather(kk, half)
+                out = tuple(
+                    out[a] + (coef(kk * 9 + a * 3) * g[0] + coef(kk * 9 + a * 3 + 1) * g[1] + coef(kk * 9 + a * 3 + 2) * g[2])
+                    for a in range(3))
+            return out
+        return lax.fori_loop(0, pn.op_rows // 27, step, (jnp.zeros((8, LN), F32),) * 3)
 
     def apply_op(phase, extra=False):
         def step(i, carry):
@@ -429,7 +466,8 @@
             vmem((pn.blocks, 256, 256), BF16),
             vmem((points, lines, LN), F32),
             vmem((points, lines, LN), I32),
-            vmem((6 * pn.qh, 256), BF16),
+            vmem((9 * pn.qh, 256), F8),
+            vmem((3 * pn.qh, LN), F32),
             vmem((3, lines, LN), F32),
             vmem((16, LN), F32),
             vmem((n, 16, LN), F32),

time: 145 us -> 120 us (0.83)
  Pallas kernels: 142 us -> 118 us
    pallas_call x1, Pallas kernels: 142 us -> 118 us  [body(): pl.pallas_call(functools.partial(kernel, pn), out_shape=(out, out), in_sp...]
where the time goes in v2:
time: 120 us
  Pallas kernels  118 us (98%)
  local copies, waits for them, and re-layouts  1.34 us (1%)
    pallas_call x1, Pallas kernels, body(): pl.pallas_call(functools.partial(kernel, pn), out_shape=(out, out), in_sp...  118 us

profile of v2, /device:TPU:1, one launch (start us, length us, event | category | flops | bytes accessed | tf_op | source)
XLA Modules:
  0.0 119.9 jit_solution(1045406927066113356)
XLA Ops:
  0.6 117.9 %solve.1 = (f32[3,8,128]{2,1,0:T(8,128)}, f32[3,8,128]{2,1,0:T(8,128)}) custom-call(f32[243,1024]{1,0:T(8,128)} %op_ref.1, f32[144,1024]{1,0:T(8,128)} %u_ref.1, f32[144,1024]{1,0:T(8,128)} %c_ref.1, f32[3,1024]{1,0:T(4,128)} %b_ref.1, s32[8,128]{1,0:T(8,128)} %bitcast.9), custom_call_target="tpu_custom_call" | custom-call | tf_op jit(solution)/shard_map/solve/pallas_call | solution.py:456
  118.5 1.3 %copy_bitcast_fusion = (f32[3,1024]{1,0:T(4,128)}, f32[3,1024]{1,0:T(4,128)}) fusion(f32[1,3,8,128]{3,2,1,0:T(8,128)} %bitcast.8, f32[1,3,8,128]{3,2,1,0:T(8,128)} %bitcast.7), kind=kLoop, calls=%fused_computation | loop fusion | bytes 49152 | tf_op jit(solution)/shard_map/reshape | solution.py:489

commit v3 on v2

--- a/solution.py
+++ b/solution.py
@@ -31,9 +31,9 @@
 
 
 def kernel(
-    pn, op_ref, u_ref, c_ref, b_ref, nr_ref, sol_ref, res_ref,
-    opd, bd, nrb, iacc, itab, kidx, qidx, tab, sinv, wd, gpk, grcv, mred, rsnd, rrcv, vsnd, vb,
-    n_s, n_r, g_s, g_r, r_s, r_r, v_s, v_r,
+    pn, op_hbm, u_hbm, c_hbm, b_ref, nr_ref, sol_ref, res_ref,
+    op_ref, u_ref, c_ref, opd, bd, nrb, inv, invb, itab, kidx, qidx, tab, sinv, wd, gpk, grcv, mred, rsnd, rrcv, vsnd, vb,
+    in_s, n_s, n_r, i_s, i_r, g_s, g_r, r_s, r_r, v_s, v_r,
 ):
     gx, gy = lax.axis_index("gx"), lax.axis_index("gy")
     me = gx * pn.ny + gy
@@ -54,11 +54,22 @@
             return 0
         lax.fori_loop(1, peers, step, 0)
 
+    def fetch(src, dst, parts, first):
+        size = src.shape[0] // 8 // parts * 8
+        copies = []
+        for i in range(parts):
+            at = pl.ds(i * size, size if i < parts - 1 else src.shape[0] - i * size)
+            copies.append(pltpu.make_async_copy(src.at[at, :], dst.at[at, :], in_s.at[first + i]))
+            copies[-1].start()
+        return copies
+
     barrier = pltpu.get_barrier_semaphore()
     others(lambda p: pl.semaphore_signal(
         barrier, inc=1, device_id=dev(p), device_id_type=pl.DeviceIdType.MESH))
 
-    lane = lax.broadcasted_iota(I32, (8, LN), 1)
+    c_in = fetch(c_hbm, c_ref, 3, 0)
+    op_in = fetch(op_hbm, op_ref, 3, 3)
+    u_in = fetch(u_hbm, u_ref, 3, 6)
     sub = lax.broadcasted_iota(I32, (8, LN), 0)
     iota_row = lax.broadcasted_iota(I32, (256, LN), 0).astype(F32).astype(BF16)
     one, zero = jnp.ones((), BF16), jnp.zeros((), BF16)
@@ -95,6 +106,8 @@
 
     nrb[me] = nr_ref[...]
 
+    for copy in c_in:
+        copy.wait()
     ext = []
     for a in range(3):
         rows_b = jnp.broadcast_to(b_ref[a : a + 1, :], (8, pn.rows))
@@ -128,51 +141,50 @@
     others(lambda p: remote(gpk, grcv.at[me], g_s.at[p], g_r.at[me], p).start())
 
     for t in range(lines):
-        at = slice(t * LN, (t + 1) * LN)
-        opd[pl.ds(t, pn.op_rows, stride=lines), :] = op_ref[:, at]
-        bd[pl.ds(t, 3, stride=lines), :] = b_ref[:, at]
+        bd[pl.ds(t, 3, stride=lines), :] = b_ref[:, t * LN : (t + 1) * LN]
     load = [bd[a * lines : (a + 1) * lines, :] for a in range(3)]
-
-    for cb in range(pn.blocks):
-        iacc[cb] = jnp.zeros((256, 256), F32)
     lane_row = lax.broadcasted_iota(I32, (1, LN), 1)
 
-    def invert_one(i):
+    def invert_one(i, acc):
         d = lax.rem(me + i, peers)
 
         @pl.when(i > 0)
         def _():
             remote(nr_ref, nrb.at[d], n_s.at[d], n_r.at[d], d).wait_recv()
 
-        zs = []
-        core = lax.rem(d, pn.ny)
-        first = (core * LN + lane_row).astype(F32).astype(BF16)
+        zs, cs = [], []
+        first = (lax.rem(d, pn.ny) * LN + lane_row).astype(F32).astype(BF16)
         for s in range(lines):
             row = nrb[d, s : s + 1, :]
             zrow = lax.bitwise_and(row, LN - 1).astype(F32).astype(BF16)
             hit = iota_row[0:LN] == zrow
-            line = lax.div(d, pn.ny) * lines + s - pn.qh
-            second = jnp.full((1, LN), 0, I32) + line
-            second = second.astype(F32).astype(BF16)
-            zs.append(jnp.concatenate([jnp.where(hit, first, zero), jnp.where(hit, second, zero)], axis=0))
+            line = jnp.zeros((1, LN), I32) + (lax.div(d, pn.ny) * lines + s - pn.qh)
+            line = line.astype(F32).astype(BF16)
+            zs.append(jnp.concatenate([jnp.where(hit, first, zero), jnp.where(hit, line, zero)], axis=0))
+            crow = jnp.clip(lax.shift_right_logical(row, 7) - me * lines, -1, lines).astype(F32).astype(BF16)
+            cs.append(jnp.where(iota_row[0:16] == crow, one, zero))
         z = jnp.concatenate(zs, axis=1)
-        for cb in range(pn.blocks):
-            cs = []
-            for s in range(lines):
-                crow = lax.shift_right_logical(nrb[d, s : s + 1, :], 7) - cb * 256
-                crow = jnp.clip(crow, -1, 256).astype(F32).astype(BF16)
-                cs.append(onehot(crow))
-            c = jnp.concatenate(cs, axis=1)
-            iacc[cb] += lax.dot_general(z, c, NT, preferred_element_type=F32)
-
-    def invert(j, _):
+        c = jnp.concatenate(cs, axis=1)
+        return acc + lax.dot_general(z, c, NT, preferred_element_type=F32)
+
+    def invert(j, acc):
         for i in range(4):
-            invert_one(4 * j + i)
-        return 0
-
-    lax.fori_loop(0, peers // 4, invert, 0)
-    for cb in range(pn.blocks):
-        itab[cb] = iacc[cb].astype(BF16)
+            acc = invert_one(4 * j + i, acc)
+        return acc
+
+    found = lax.fori_loop(0, peers // 4, invert, jnp.zeros((2 * LN, 16), F32))
+    found = jnp.concatenate([found, jnp.zeros((2 * LN, LN - 16), F32)], axis=1)
+    first = jnp.transpose(found[0:LN])[0:lines]
+    line = jnp.transpose(found[LN:])[0:lines]
+    code = first + 256.0 * (line + 1.0 * pn.qh)
+    inv[...] = code
+    invb[me] = code
+    others(lambda p: remote(inv, invb.at[me], i_s.at[p], i_r.at[me], p).start())
+
+    for copy in op_in + u_in:
+        copy.wait()
+    for t in range(lines):
+        opd[pl.ds(t, pn.op_rows, stride=lines), :] = op_ref[:, t * LN : (t + 1) * LN]
 
     others(lambda p: remote(gpk, grcv.at[p], g_s.at[p], g_r.at[p], p).wait_recv())
     total = grcv[0]
@@ -197,13 +209,17 @@
     lower = jnp.logical_or(diag, lanes_e <= rows_e)
     mat = jnp.where(jnp.logical_or(lower, lanes_e == k), low, high)
     mat = jnp.where(jnp.logical_and(rows_e == k, lanes_e < k), high, mat)
-    for i in range(k):
-        row = mat[i : i + 1, :]
-        col = jnp.broadcast_to(mat[:, i : i + 1], (ke, LN))
-        at = lanes_e == i
-        scaled = jnp.where(lane_row == i, 1.0, row) / col[i : i + 1]
-        inner = jnp.where(at, 0.0, mat) - col * scaled
-        mat = jnp.where(rows_e == i, scaled, inner)
+    for i in range(0, k, 2):
+        c0 = jnp.broadcast_to(mat[:, i : i + 1], (ke, LN))
+        c1 = jnp.broadcast_to(mat[:, i + 1 : i + 2], (ke, LN))
+        r0 = jnp.where(lane_row == i, 1.0, jnp.where(lane_row == i + 1, 0.0, mat[i : i + 1]))
+        r1 = jnp.where(lane_row == i + 1, 1.0, jnp.where(lane_row == i, 0.0, mat[i + 1 : i + 2]))
+        over = 1.0 / c0[i : i + 1]
+        up, down = c1[i : i + 1] * over, c0[i + 1 : i + 2] * over
+        s1 = (r1 - down * r0) / (c1[i + 1 : i + 2] - c0[i + 1 : i + 2] * up)
+        s0 = r0 * over - up * s1
+        inner = jnp.where(lax.div(lanes_e, 2) == i // 2, 0.0, mat) - c0 * s0 - c1 * s1
+        mat = jnp.where(rows_e == i, s0, jnp.where(rows_e == i + 1, s1, inner))
     ginv = jnp.where(lanes_e < k, mat, 0.0)[0:k]
     z0 = jnp.broadcast_to(mat[0:k, k : k + 1], (k, LN))
     beta = jnp.sqrt(jnp.broadcast_to(mat[k : k + 1, k : k + 1], (1, LN)))
@@ -222,6 +238,7 @@
         return out
 
     half_n = pn.nx // 2
+    half_w = half_n * pn.ny
     side = lax.div(gx, half_n)
 
     def spread(phase, v):
@@ -229,39 +246,56 @@
             vsnd[phase, a] = v[a]
             vb[phase, gy, a, pl.ds(pl.multiple_of(gx * lines, 8), 8), :] = v[a]
         mine = pl.ds(pl.multiple_of(gx * lines, 8), 8)
-        half = half_n * pn.ny
-        at = me - side * half
-
         def send(p):
             remote(vsnd.at[phase], vb.at[phase, gy, :, mine, :], v_s.at[phase, p], v_r.at[phase, me], p).start()
 
         def near(i, _):
-            send(side * half + lax.rem(at + i, half))
+            send(side * half_w + lax.rem(me - side * half_w + i, half_w))
             return 0
 
         def far(i, _):
-            send((1 - side) * half + lax.rem(at + i, half))
+            send(((1 - side) * half_n + lax.rem(gx - side * half_n + i, half_n)) * pn.ny + gy)
             return 0
 
-        lax.fori_loop(1, half, near, 0)
-        lax.fori_loop(0, half, far, 0)
+        lax.fori_loop(0, half_n, far, 0)
+        lax.fori_loop(1, half_w, near, 0)
+
+    def block(phase, p):
+        at = pl.ds(pl.multiple_of(lax.div(p, pn.ny) * lines, 8), 8)
+        return vb.at[phase, lax.rem(p, pn.ny), :, at, :]
+
+    def come(phase, p):
+        remote(vsnd.at[phase], block(phase, p), v_s.at[phase, p], v_r.at[phase, p], p).wait_recv()
+
+    def far_chip(i):
+        return jnp.where(side == 0, half_n + i, half_n - 1 - i)
+
+    def relay(phase, i):
+        p = far_chip(i) * pn.ny + gy
+        come(phase, p)
+        other = far_chip(i) * pn.ny + 1 - gy
+        remote(block(phase, p), block(phase, p), v_s.at[phase, other], v_r.at[phase, p], gx * pn.ny + 1 - gy).start()
 
     def arrive(phase, half):
-        def step(i, _):
-            p = half * half_n * pn.ny + i
-            at = pl.ds(pl.multiple_of(lax.div(p, pn.ny) * lines, 8), 8)
-
-            @pl.when(p != me)
-            def _():
-                remote(vsnd.at[phase], vb.at[phase, lax.rem(p, pn.ny), :, at, :],
-                       v_s.at[phase, p], v_r.at[phase, p], p).wait_recv()
-            return 0
-        lax.fori_loop(0, half_n * pn.ny, step, 0)
+        @pl.when(half == side)
+        def _():
+            def step(i, _):
+                come(phase, side * half_w + lax.rem(me - side * half_w + i, half_w))
+                return 0
+            lax.fori_loop(1, half_w, step, 0)
+
+        @pl.when(half != side)
+        def _():
+            def step(i, _):
+                come(phase, far_chip(i) * pn.ny + 1 - gy)
+                return 0
+            lax.fori_loop(0, half_n, step, 0)
+
         begin = pl.ds(pl.multiple_of(half * pn.qh, 8), pn.qh)
         for b in range(3):
             xs = [vb[phase, core, b, begin, :] for core in range(pn.ny)]
             top = functools.reduce(jnp.maximum, [jnp.abs(x) for x in xs])
-            top = jnp.maximum(jnp.max(top, axis=1, keepdims=True), 1e-30)
+            top = jnp.maximum(jnp.max(top, axis=1, keepdims=True), 1e-36)
             scale = 240.0 / top
             sinv[b * pn.qh : (b + 1) * pn.qh, :] = jnp.broadcast_to(top * (1.0 / 240.0), (pn.qh, LN))
             for core in range(pn.ny):
@@ -298,8 +332,15 @@
     def coef(i):
         return opd[pl.ds(pl.multiple_of(i * lines, 8), 8), :]
 
-    def apply_half(half):
+    turns = pn.op_rows // 27
+    per_turn = -(-half_n // (turns - 1))
+
+    def apply_half(phase, half):
         def step(i, out):
+            for j in range(per_turn):
+                @pl.when(jnp.logical_and(half == side, i * per_turn + j < half_n))
+                def _():
+                    relay(phase, i * per_turn + j)
             for u in range(3):
                 kk = 3 * i + u
                 g = gather(kk, half)
@@ -307,13 +348,13 @@
                     out[a] + (coef(kk * 9 + a * 3) * g[0] + coef(kk * 9 + a * 3 + 1) * g[1] + coef(kk * 9 + a * 3 + 2) * g[2])
                     for a in range(3))
             return out
-        return lax.fori_loop(0, pn.op_rows // 27, step, (jnp.zeros((8, LN), F32),) * 3)
+        return lax.fori_loop(0, turns, step, (jnp.zeros((8, LN), F32),) * 3)
 
     def apply_op(phase, extra=False):
         def step(i, carry):
             half = lax.rem(side + i, 2)
             arrive(phase, half)
-            part = apply_half(half)
+            part = apply_half(phase, half)
             if extra:
                 part = part + tuple(gather(pn.op_rows // 9, half))
             return tuple(x + y for x, y in zip(carry, part))
@@ -354,6 +395,11 @@
     v1 = [(load[a] - part[a]) / beta for a in range(3)]
     spread(0, v1)
 
+    others(lambda p: remote(inv, invb.at[p], i_s.at[p], i_r.at[p], p).wait_recv())
+    for cb in range(pn.blocks):
+        codes = invb[cb * 256 // lines : (cb + 1) * 256 // lines].reshape(256, LN).astype(I32)
+        itab[cb, 0:LN, :] = jnp.transpose(lax.bitwise_and(codes, 255).astype(F32)).astype(BF16)
+        itab[cb, LN:, :] = jnp.transpose((lax.shift_right_logical(codes, 8) - pn.qh).astype(F32)).astype(BF16)
     nr = nr_ref[...]
     x_at = lax.div(nr, pn.height * LN)
     y_at = lax.bitwise_and(lax.shift_right_logical(nr, 7), pn.height - 1)
@@ -426,6 +472,12 @@
     for a in range(3):
         sol_ref[a] = out[3 + a]
 
+    def pass_on(i, _):
+        relay(3, i)
+        return 0
+
+    lax.fori_loop(0, half_n, pass_on, 0)
+
     def last(i, carry):
         half = lax.rem(side + i, 2)
         arrive(3, half)
@@ -437,6 +489,7 @@
 
     others(lambda p: remote(nr_ref, nrb.at[me], n_s.at[p], n_r.at[me], p).wait_send())
     others(lambda p: remote(gpk, grcv.at[me], g_s.at[p], g_r.at[me], p).wait_send())
+    others(lambda p: remote(inv, invb.at[me], i_s.at[p], i_r.at[me], p).wait_send())
     mine = pl.ds(pl.multiple_of(gx * lines, 8), 8)
     for phase in range(2):
         others(lambda p: remote(rsnd.at[phase], rrcv.at[phase, me], r_s.at[phase, p], r_r.at[phase, me], p).wait_send())
@@ -456,13 +509,17 @@
     sol, res = pl.pallas_call(
         functools.partial(kernel, pn),
         out_shape=(out, out),
-        in_specs=[whole] * 5,
+        in_specs=[pl.BlockSpec(memory_space=pl.ANY)] * 3 + [whole] * 2,
         out_specs=(whole, whole),
         scratch_shapes=[
+            vmem((pn.op_rows, rows), F32),
+            vmem((pn.basis_rows, rows), F32),
+            vmem((pn.basis_rows, rows), F32),
             vmem((pn.op_rows * lines, LN), F32),
             vmem((3 * lines, LN), F32),
             vmem((n, lines, LN), I32),
-            vmem((pn.blocks, 256, 256), F32),
+            vmem((lines, LN), F32),
+            vmem((n, lines, LN), F32),
             vmem((pn.blocks, 256, 256), BF16),
             vmem((points, lines, LN), F32),
             vmem((points, lines, LN), I32),
@@ -476,6 +533,8 @@
             vmem((2, n, 1, LN), F32),
             vmem((4, 3, lines, LN), F32),
             vmem((4, ny, 3, pn.q, LN), F32),
+            dma((9,)),
+            dma((n,)), dma((n,)),
             dma((n,)), dma((n,)),
             dma((n,)), dma((n,)),
             dma((2, n)), dma((2, n)),

time: 120 us -> 116 us (0.967)
  Pallas kernels: 118 us -> 114 us
    pallas_call x1, Pallas kernels: 118 us -> 114 us  [body(): pl.pallas_call(functools.partial(kernel, pn), out_shape=(out, out), in_sp...]
where the time goes in v3:
time: 116 us
  Pallas kernels  114 us (98%)
  local copies, waits for them, and re-layouts  1.34 us (1%)
    pallas_call x1, Pallas kernels, body(): pl.pallas_call(functools.partial(kernel, pn), out_shape=(out, out), in_sp...  114 us

profile of v3, /device:TPU:1, one launch (start us, length us, event | category | flops | bytes accessed | tf_op | source)
XLA Modules:
  0.0 115.7 jit_solution(17708868970883861438)
XLA Ops:
  0.6 113.7 %solve.1 = (f32[3,8,128]{2,1,0:T(8,128)}, f32[3,8,128]{2,1,0:T(8,128)}) custom-call(f32[243,1024]{1,0:T(8,128)} %op_hbm.1, f32[144,1024]{1,0:T(8,128)} %u_hbm.1, f32[144,1024]{1,0:T(8,128)} %c_hbm.1, f32[3,1024]{1,0:T(4,128)} %b_ref.1, s32[8,128]{1,0:T(8,128)} %bitcast.9), custom_call_target="tpu_custom_call" | custom-call | tf_op jit(solution)/shard_map/solve/pallas_call | solution.py:509
  114.3 1.3 %copy_bitcast_fusion = (f32[3,1024]{1,0:T(4,128)}, f32[3,1024]{1,0:T(4,128)}) fusion(f32[1,3,8,128]{3,2,1,0:T(8,128)} %bitcast.8, f32[1,3,8,128]{3,2,1,0:T(8,128)} %bitcast.7), kind=kLoop, calls=%fused_computation | loop fusion | bytes 49152 | tf_op jit(solution)/shard_map/reshape | solution.py:548

commit v4 on v3

--- a/solution.py
+++ b/solution.py
@@ -33,7 +33,7 @@
 def kernel(
     pn, op_hbm, u_hbm, c_hbm, b_ref, nr_ref, sol_ref, res_ref,
     op_ref, u_ref, c_ref, opd, bd, nrb, inv, invb, itab, kidx, qidx, tab, sinv, wd, gpk, grcv, mred, rsnd, rrcv, vsnd, vb,
-    in_s, n_s, n_r, i_s, i_r, g_s, g_r, r_s, r_r, v_s, v_r,
+in_s, n_s, n_r, i_s, i_r, g_s, g_r, r_s, r_r, near_s, far_s, pass_s, near_r, far_r, pass_r,
 ):
     gx, gy = lax.axis_index("gx"), lax.axis_index("gy")
     me = gx * pn.ny + gy
@@ -54,22 +54,23 @@
             return 0
         lax.fori_loop(1, peers, step, 0)
 
-    def fetch(src, dst, parts, first):
-        size = src.shape[0] // 8 // parts * 8
-        copies = []
-        for i in range(parts):
-            at = pl.ds(i * size, size if i < parts - 1 else src.shape[0] - i * size)
-            copies.append(pltpu.make_async_copy(src.at[at, :], dst.at[at, :], in_s.at[first + i]))
-            copies[-1].start()
-        return copies
+    def fetch(src, dst, i):
+        copy = pltpu.make_async_copy(src, dst, in_s.at[i])
+        copy.start()
+        return copy
+
+    def all_of(ref, ssem, rsem):
+        return remote(ref, ref, ssem, rsem, lax.rem(me + 1, peers))
+
+    most = pl.ds(0, peers - 1)
 
     barrier = pltpu.get_barrier_semaphore()
     others(lambda p: pl.semaphore_signal(
         barrier, inc=1, device_id=dev(p), device_id_type=pl.DeviceIdType.MESH))
 
-    c_in = fetch(c_hbm, c_ref, 3, 0)
-    op_in = fetch(op_hbm, op_ref, 3, 3)
-    u_in = fetch(u_hbm, u_ref, 3, 6)
+    c_in = fetch(c_hbm, c_ref, 0)
+    op_in = fetch(op_hbm, op_ref, 1)
+    u_in = fetch(u_hbm, u_ref, 2)
     sub = lax.broadcasted_iota(I32, (8, LN), 0)
     iota_row = lax.broadcasted_iota(I32, (256, LN), 0).astype(F32).astype(BF16)
     one, zero = jnp.ones((), BF16), jnp.zeros((), BF16)
@@ -106,8 +107,7 @@
 
     nrb[me] = nr_ref[...]
 
-    for copy in c_in:
-        copy.wait()
+    c_in.wait()
     ext = []
     for a in range(3):
         rows_b = jnp.broadcast_to(b_ref[a : a + 1, :], (8, pn.rows))
@@ -137,8 +137,8 @@
     grcv[me] = packet
 
     pl.semaphore_wait(barrier, peers - 1)
-    others(lambda p: remote(nr_ref, nrb.at[me], n_s.at[p], n_r.at[me], p).start())
-    others(lambda p: remote(gpk, grcv.at[me], g_s.at[p], g_r.at[me], p).start())
+    others(lambda p: remote(nr_ref, nrb.at[me], n_s, n_r, p).start())
+    others(lambda p: remote(gpk, grcv.at[me], g_s, g_r, p).start())
 
     for t in range(lines):
         bd[pl.ds(t, 3, stride=lines), :] = b_ref[:, t * LN : (t + 1) * LN]
@@ -146,12 +146,7 @@
     lane_row = lax.broadcasted_iota(I32, (1, LN), 1)
 
     def invert_one(i, acc):
-        d = lax.rem(me + i, peers)
-
-        @pl.when(i > 0)
-        def _():
-            remote(nr_ref, nrb.at[d], n_s.at[d], n_r.at[d], d).wait_recv()
-
+        d = i
         zs, cs = [], []
         first = (lax.rem(d, pn.ny) * LN + lane_row).astype(F32).astype(BF16)
         for s in range(lines):
@@ -172,6 +167,7 @@
             acc = invert_one(4 * j + i, acc)
         return acc
 
+    all_of(nrb.at[most], n_s, n_r).wait_recv()
     found = lax.fori_loop(0, peers // 4, invert, jnp.zeros((2 * LN, 16), F32))
     found = jnp.concatenate([found, jnp.zeros((2 * LN, LN - 16), F32)], axis=1)
     first = jnp.transpose(found[0:LN])[0:lines]
@@ -179,14 +175,14 @@
     code = first + 256.0 * (line + 1.0 * pn.qh)
     inv[...] = code
     invb[me] = code
-    others(lambda p: remote(inv, invb.at[me], i_s.at[p], i_r.at[me], p).start())
-
-    for copy in op_in + u_in:
-        copy.wait()
+    others(lambda p: remote(inv, invb.at[me], i_s, i_r, p).start())
+
+    op_in.wait()
+    u_in.wait()
     for t in range(lines):
         opd[pl.ds(t, pn.op_rows, stride=lines), :] = op_ref[:, t * LN : (t + 1) * LN]
 
-    others(lambda p: remote(gpk, grcv.at[p], g_s.at[p], g_r.at[p], p).wait_recv())
+    all_of(grcv.at[most], g_s, g_r).wait_recv()
     total = grcv[0]
     for d in range(1, peers):
         total = total + grcv[d]
@@ -246,15 +242,15 @@
             vsnd[phase, a] = v[a]
             vb[phase, gy, a, pl.ds(pl.multiple_of(gx * lines, 8), 8), :] = v[a]
         mine = pl.ds(pl.multiple_of(gx * lines, 8), 8)
-        def send(p):
-            remote(vsnd.at[phase], vb.at[phase, gy, :, mine, :], v_s.at[phase, p], v_r.at[phase, me], p).start()
-
         def near(i, _):
-            send(side * half_w + lax.rem(me - side * half_w + i, half_w))
+            p = (side * half_w + lax.rem(me - side * half_w + i, half_w))
+            remote(vsnd.at[phase], vb.at[phase, gy, :, mine, :], near_s.at[phase], near_r.at[phase], p).start()
             return 0
 
         def far(i, _):
-            send(((1 - side) * half_n + lax.rem(gx - side * half_n + i, half_n)) * pn.ny + gy)
+            p = ((1 - side) * half_n + lax.rem(gx - side * half_n + i, half_n)) * pn.ny + gy
+            remote(vsnd.at[phase], vb.at[phase, gy, :, mine, :], far_s.at[phase],
+                   far_r.at[phase, gx - side * half_n], p).start()
             return 0
 
         lax.fori_loop(0, half_n, far, 0)
@@ -264,32 +260,23 @@
         at = pl.ds(pl.multiple_of(lax.div(p, pn.ny) * lines, 8), 8)
         return vb.at[phase, lax.rem(p, pn.ny), :, at, :]
 
-    def come(phase, p):
-        remote(vsnd.at[phase], block(phase, p), v_s.at[phase, p], v_r.at[phase, p], p).wait_recv()
-
-    def far_chip(i):
-        return jnp.where(side == 0, half_n + i, half_n - 1 - i)
+    def rows_of(count):
+        return opd.at[pl.ds(0, count * 3 * lines), :]
 
     def relay(phase, i):
-        p = far_chip(i) * pn.ny + gy
-        come(phase, p)
-        other = far_chip(i) * pn.ny + 1 - gy
-        remote(block(phase, p), block(phase, p), v_s.at[phase, other], v_r.at[phase, p], gx * pn.ny + 1 - gy).start()
+        at = jnp.where(side == 0, i, half_n - 1 - i)
+        p = ((1 - side) * half_n + at) * pn.ny + gy
+        remote(vsnd.at[phase], block(phase, p), far_s.at[phase], far_r.at[phase, at], p).wait_recv()
+        remote(block(phase, p), block(phase, p), pass_s.at[phase], pass_r.at[phase], gx * pn.ny + 1 - gy).start()
 
     def arrive(phase, half):
         @pl.when(half == side)
         def _():
-            def step(i, _):
-                come(phase, side * half_w + lax.rem(me - side * half_w + i, half_w))
-                return 0
-            lax.fori_loop(1, half_w, step, 0)
+            all_of(rows_of(half_w - 1), near_s.at[phase], near_r.at[phase]).wait_recv()
 
         @pl.when(half != side)
         def _():
-            def step(i, _):
-                come(phase, far_chip(i) * pn.ny + 1 - gy)
-                return 0
-            lax.fori_loop(0, half_n, step, 0)
+            all_of(rows_of(half_n), pass_s.at[phase], pass_r.at[phase]).wait_recv()
 
         begin = pl.ds(pl.multiple_of(half * pn.qh, 8), pn.qh)
         for b in range(3):
@@ -382,8 +369,8 @@
         mine_row = lax.dot_general(jnp.ones((8, LN), F32), mred[...], NT, precision=HIGH, preferred_element_type=F32)[0:1]
         rsnd[phase] = mine_row
         rrcv[phase, me] = mine_row
-        others(lambda p: remote(rsnd.at[phase], rrcv.at[phase, me], r_s.at[phase, p], r_r.at[phase, me], p).start())
-        others(lambda p: remote(rsnd.at[phase], rrcv.at[phase, p], r_s.at[phase, p], r_r.at[phase, p], p).wait_recv())
+        others(lambda p: remote(rsnd.at[phase], rrcv.at[phase, me], r_s.at[phase], r_r.at[phase], p).start())
+        all_of(rrcv.at[phase, most], r_s.at[phase], r_r.at[phase]).wait_recv()
         prow = jnp.sum(rrcv[phase], axis=0)
         pcol = lsum(jnp.where(lanes_e == rows_e, prow, 0.0))
         z = lsum(ginv * prow)
@@ -395,7 +382,7 @@
     v1 = [(load[a] - part[a]) / beta for a in range(3)]
     spread(0, v1)
 
-    others(lambda p: remote(inv, invb.at[p], i_s.at[p], i_r.at[p], p).wait_recv())
+    all_of(invb.at[most], i_s, i_r).wait_recv()
     for cb in range(pn.blocks):
         codes = invb[cb * 256 // lines : (cb + 1) * 256 // lines].reshape(256, LN).astype(I32)
         itab[cb, 0:LN, :] = jnp.transpose(lax.bitwise_and(codes, 255).astype(F32)).astype(BF16)
@@ -487,15 +474,15 @@
     for a in range(3):
         res_ref[a] = out[a]
 
-    others(lambda p: remote(nr_ref, nrb.at[me], n_s.at[p], n_r.at[me], p).wait_send())
-    others(lambda p: remote(gpk, grcv.at[me], g_s.at[p], g_r.at[me], p).wait_send())
-    others(lambda p: remote(inv, invb.at[me], i_s.at[p], i_r.at[me], p).wait_send())
-    mine = pl.ds(pl.multiple_of(gx * lines, 8), 8)
+    all_of(nrb.at[most], n_s, n_r).wait_send()
+    all_of(grcv.at[most], g_s, g_r).wait_send()
+    all_of(invb.at[most], i_s, i_r).wait_send()
     for phase in range(2):
-        others(lambda p: remote(rsnd.at[phase], rrcv.at[phase, me], r_s.at[phase, p], r_r.at[phase, me], p).wait_send())
+        all_of(rrcv.at[phase, most], r_s.at[phase], r_r.at[phase]).wait_send()
     for phase in range(4):
-        others(lambda p: remote(
-            vsnd.at[phase], vb.at[phase, gy, :, mine, :], v_s.at[phase, p], v_r.at[phase, me], p).wait_send())
+        all_of(rows_of(half_w - 1), near_s.at[phase], near_r.at[phase]).wait_send()
+        all_of(rows_of(half_n), far_s.at[phase], pass_r.at[phase]).wait_send()
+        all_of(rows_of(half_n), pass_s.at[phase], pass_r.at[phase]).wait_send()
 
 
 def body(nx, ny, operator, basis_u, basis_c, right_side, new_rows):
@@ -533,12 +520,11 @@
             vmem((2, n, 1, LN), F32),
             vmem((4, 3, lines, LN), F32),
             vmem((4, ny, 3, pn.q, LN), F32),
-            dma((9,)),
-            dma((n,)), dma((n,)),
-            dma((n,)), dma((n,)),
-            dma((n,)), dma((n,)),
-            dma((2, n)), dma((2, n)),
-            dma((4, n)), dma((4, n)),
+            dma((3,)),
+            dma, dma, dma, dma, dma, dma,
+            dma((2,)), dma((2,)),
+            dma((4,)), dma((4,)), dma((4,)),
+            dma((4,)), dma((4, nx // 2)), dma((4,)),
         ],
         compiler_params=pltpu.CompilerParams(
             collective_id=0, has_side_effects=True, vmem_limit_bytes=60 << 20

time: 116 us -> 103 us (0.89)
  Pallas kernels: 114 us -> 101 us
    pallas_call x1, Pallas kernels: 114 us -> 101 us  [body(): pl.pallas_call(functools.partial(kernel, pn), out_shape=(out, out), in_sp...]
where the time goes in v4:
time: 103 us
  Pallas kernels  101 us (98%)
  local copies, waits for them, and re-layouts  1.34 us (1%)
    pallas_call x1, Pallas kernels, body(): pl.pallas_call(functools.partial(kernel, pn), out_shape=(out, out), in_sp...  101 us

profile of v4, /device:TPU:1, one launch (start us, length us, event | category | flops | bytes accessed | tf_op | source)
XLA Modules:
  0.0 102.5 jit_solution(2111742797457394043)
XLA Ops:
  0.6 100.6 %solve.1 = (f32[3,8,128]{2,1,0:T(8,128)}, f32[3,8,128]{2,1,0:T(8,128)}) custom-call(f32[243,1024]{1,0:T(8,128)} %op_hbm.1, f32[144,1024]{1,0:T(8,128)} %u_hbm.1, f32[144,1024]{1,0:T(8,128)} %c_hbm.1, f32[3,1024]{1,0:T(4,128)} %b_ref.1, s32[8,128]{1,0:T(8,128)} %bitcast.9), custom_call_target="tpu_custom_call" | custom-call | tf_op jit(solution)/shard_map/solve/pallas_call | solution.py:496
  101.2 1.3 %copy_bitcast_fusion = (f32[3,1024]{1,0:T(4,128)}, f32[3,1024]{1,0:T(4,128)}) fusion(f32[1,3,8,128]{3,2,1,0:T(8,128)} %bitcast.8, f32[1,3,8,128]{3,2,1,0:T(8,128)} %bitcast.7), kind=kLoop, calls=%fused_computation | loop fusion | bytes 49152 | tf_op jit(solution)/shard_map/reshape | solution.py:534

commit v5 on v4

--- a/solution.py
+++ b/solution.py
@@ -167,6 +167,10 @@
             acc = invert_one(4 * j + i, acc)
         return acc
 
+    op_in.wait()
+    u_in.wait()
+    for t in range(lines):
+        opd[pl.ds(t, pn.op_rows, stride=lines), :] = op_ref[:, t * LN : (t + 1) * LN]
     all_of(nrb.at[most], n_s, n_r).wait_recv()
     found = lax.fori_loop(0, peers // 4, invert, jnp.zeros((2 * LN, 16), F32))
     found = jnp.concatenate([found, jnp.zeros((2 * LN, LN - 16), F32)], axis=1)
@@ -177,10 +181,6 @@
     invb[me] = code
     others(lambda p: remote(inv, invb.at[me], i_s, i_r, p).start())
 
-    op_in.wait()
-    u_in.wait()
-    for t in range(lines):
-        opd[pl.ds(t, pn.op_rows, stride=lines), :] = op_ref[:, t * LN : (t + 1) * LN]
 
     all_of(grcv.at[most], g_s, g_r).wait_recv()
     total = grcv[0]
@@ -253,8 +253,11 @@
                    far_r.at[phase, gx - side * half_n], p).start()
             return 0
 
-        lax.fori_loop(0, half_n, far, 0)
+        if phase == 3:
+            lax.fori_loop(0, half_n, far, 0)
         lax.fori_loop(1, half_w, near, 0)
+        if phase < 3:
+            lax.fori_loop(0, half_n, far, 0)
 
     def block(phase, p):
         at = pl.ds(pl.multiple_of(lax.div(p, pn.ny) * lines, 8), 8)
@@ -386,7 +389,8 @@
     for cb in range(pn.blocks):
         codes = invb[cb * 256 // lines : (cb + 1) * 256 // lines].reshape(256, LN).astype(I32)
         itab[cb, 0:LN, :] = jnp.transpose(lax.bitwise_and(codes, 255).astype(F32)).astype(BF16)
-        itab[cb, LN:, :] = jnp.transpose((lax.shift_right_logical(codes, 8) - pn.qh).astype(F32)).astype(BF16)
+        line = (lax.shift_right_logical(codes, 8) - pn.qh) * 256
+        itab[cb, LN:, :] = jnp.transpose(line.astype(F32)).astype(BF16)
     nr = nr_ref[...]
     x_at = lax.div(nr, pn.height * LN)
     y_at = lax.bitwise_and(lax.shift_right_logical(nr, 7), pn.height - 1)
@@ -394,24 +398,25 @@
     zl = LN.bit_length() - 4
 
     def look(crow_of, zrow_of, shifts):
-        vals = [[[None] * lines for _ in range(2)] for _ in shifts]
+        vals = [[None] * lines for _ in shifts]
         for c in range(lines // 2):
             r = None
             for cb in range(pn.blocks):
                 w = jnp.concatenate(
                     [onehot(jnp.clip(crow_of(2 * c + t) - cb * 256, -1, 256).astype(F32).astype(BF16)) for t in range(2)],
                     axis=1)
-                d = jnp.dot(itab[cb], w, preferred_element_type=F32)
-                r = d if r is None else r + d
+                for p in range(2):
+                    d = jnp.dot(itab[cb, p * LN : (p + 1) * LN, :], w, preferred_element_type=F32)
+                    r = d if r is None else r + d
             for t in range(2):
                 for i, dz in enumerate(shifts):
                     zq = jnp.broadcast_to(zrow_of(2 * c + t), (8, LN)) + dz
                     bits = [lax.bitwise_and(zq, 8 << j) != 0 for j in range(zl)]
                     here = lax.bitwise_and(zq, 7) == sub
-                    for p in range(2):
-                        parts = [r[p * LN + 8 * j : p * LN + 8 * j + 8, t * LN : (t + 1) * LN] for j in range(LN // 8)]
-                        vals[i][p][2 * c + t] = jnp.where(here, pick(parts, bits), 0.0)
-        return [[fold(vals[i][p]) for p in range(2)] for i in range(len(shifts))]
+                    parts = [r[8 * j : 8 * j + 8, t * LN : (t + 1) * LN] for j in range(LN // 8)]
+                    vals[i][2 * c + t] = jnp.where(here, pick(parts, bits), 0.0)
+        codes = [fold(vals[i]).astype(I32) + 256 * pn.qh for i in range(len(shifts))]
+        return [(lax.bitwise_and(v, 255).astype(F32), lax.shift_right_arithmetic(v, 8)) for v in codes]
 
     def neighbours(j, _):
         dx = lax.div(j, 3) - 1
@@ -427,14 +432,14 @@
             zs = z_at + dz
             good = jnp.logical_and(inside, jnp.logical_and(zs >= 0, zs < LN))
             kidx[j * 3 + i] = found[i][0]
-            qidx[j * 3 + i] = jnp.where(good, found[i][1].astype(I32) + pn.qh, -1)
+            qidx[j * 3 + i] = jnp.where(good, found[i][1], -1)
         return 0
 
     lax.fori_loop(0, 9, neighbours, 0)
     own = look(
         lambda t: jnp.zeros((1, LN), I32) + (me * lines + t), lambda t: lane_row, (0,))
     kidx[pn.op_rows // 9] = own[0][0]
-    qidx[pn.op_rows // 9] = own[0][1].astype(I32) + pn.qh
+    qidx[pn.op_rows // 9] = own[0][1]
 
     w1 = apply_op(0)
     z1, pz, (h11, ww, _) = sums_of(0, w1, [v1])

time: 103 us -> 102 us (level)
  Pallas kernels: 101 us -> 99.5 us
    pallas_call x1, Pallas kernels: 101 us -> 99.5 us  [body(): pl.pallas_call(functools.partial(kernel, pn), out_shape=(out, out), in_sp...]
where the time goes in v5:
time: 102 us; the launch traced here: 101 us
  Pallas kernels  99.5 us (98%)
  local copies, waits for them, and re-layouts  1.34 us (1%)
    pallas_call x1, Pallas kernels, body(): pl.pallas_call(functools.partial(kernel, pn), out_shape=(out, out), in_sp...  99.5 us

profile of v5, /device:TPU:1, one launch (start us, length us, event | category | flops | bytes accessed | tf_op | source)
XLA Modules:
  0.0 101.4 jit_solution(12225538880384579158)
XLA Ops:
  0.6 99.5 %solve.1 = (f32[3,8,128]{2,1,0:T(8,128)}, f32[3,8,128]{2,1,0:T(8,128)}) custom-call(f32[243,1024]{1,0:T(8,128)} %op_hbm.1, f32[144,1024]{1,0:T(8,128)} %u_hbm.1, f32[144,1024]{1,0:T(8,128)} %c_hbm.1, f32[3,1024]{1,0:T(4,128)} %b_ref.1, s32[8,128]{1,0:T(8,128)} %bitcast.9), custom_call_target="tpu_custom_call" | custom-call | tf_op jit(solution)/shard_map/solve/pallas_call | solution.py:501
  100.1 1.3 %copy_bitcast_fusion = (f32[3,1024]{1,0:T(4,128)}, f32[3,1024]{1,0:T(4,128)}) fusion(f32[1,3,8,128]{3,2,1,0:T(8,128)} %bitcast.8, f32[1,3,8,128]{3,2,1,0:T(8,128)} %bitcast.7), kind=kLoop, calls=%fused_computation | loop fusion | bytes 49152 | tf_op jit(solution)/shard_map/reshape | solution.py:539
